TPU v7x, 32 devices: a whole 2x2x4 slice. The times are simulated.
32 devices in a mesh: row: 4 (over x, core), col: 8 (over z, y).
Axes of the slice: x: 2, y: 2, z: 4, core: 2. Of those that a mesh axis runs over, the one named last changes fastest.
Arguments:
- tokens: bfloat16 [1024, 4096], P('col', 'row'), may hold values from -12 to 12
- target: bfloat16 [1024, 4096], P('col', 'row'), may hold values from -6 to 6
- gate_weight: bfloat16 [4096, 5504], P('row', 'col'), may hold values from -0.09375 to 0.09375
- up_weight: bfloat16 [4096, 5504], P('row', 'col'), may hold values from -0.09375 to 0.09375
- down_weight: bfloat16 [5504, 4096], P('col', 'row'), may hold values from -0.078125 to 0.078125
- probe_gate: int32 [4096, 5504], P('row', 'col'), may hold values from 0 to 1
- probe_up: int32 [4096, 5504], P('row', 'col'), may hold values from 0 to 1
- probe_down: int32 [5504, 4096], P('col', 'row'), may hold values from 0 to 1
- first_gate: float32 [4096, 5504], P('row', 'col'), may hold values from -1.8 to 1.8
- first_up: float32 [4096, 5504], P('row', 'col'), may hold values from -1.8 to 1.8
- first_down: float32 [5504, 4096], P('col', 'row'), may hold values from -1.8 to 1.8
- second_gate: float32 [4096, 5504], P('row', 'col'), may hold values from 0.01 to 0.2
- second_up: float32 [4096, 5504], P('row', 'col'), may hold values from 0.01 to 0.2
- second_down: float32 [5504, 4096], P('col', 'row'), may hold values from 0.01 to 0.2
Outputs:
- new_first_gate: float32 [4096, 5504], P('row', 'col')
- new_first_up: float32 [4096, 5504], P('row', 'col')
- new_first_down: float32 [5504, 4096], P('col', 'row')
- new_second_gate: float32 [4096, 5504], P('row', 'col')
- new_second_up: float32 [4096, 5504], P('row', 'col')
- new_second_down: float32 [5504, 4096], P('col', 'row')
- update_gate: float32 [4096, 5504], P('row', 'col')
- update_up: float32 [4096, 5504], P('row', 'col')
- update_down: float32 [5504, 4096], P('col', 'row')
Inputs may be any that keep to these rules, and one draw needn't show every extreme that they name: `probe_gate`: probe bits; the probe is 2 p - 1. `probe_up`: probe bits; the probe is 2 p - 1. `probe_down`: probe bits; the probe is 2 p - 1.
All inputs are finite; a program needn't handle non-finite values.
Results may differ from a plain program's by a relative error of at most 0.038.
Values may be sent and summed in bfloat16 or wider, within the bound.
No kernel may reach another device: no remote copies, remote signals or barrier semaphores. Data moves between devices by JAX's collectives and lax.ppermute only.
A program may use at most 256 MiB of HBM per device.

v0:
```python
import jax
import jax.numpy as jnp
from jax import lax
from jax.sharding import PartitionSpec as P

D = 4096
FF = 5504
STEP = 10


def activation(pre):
    sig = jax.nn.sigmoid(pre)
    act = pre * sig
    slope = sig * (1.0 + pre * (1.0 - sig))
    bend = sig * (1.0 - sig) * (2.0 + pre * (1.0 - 2.0 * sig))
    return (act, slope, bend)


def block_mean(values):
    height, breadth = values.shape
    means = values.reshape(height // 4, 4, breadth // 4, 4).mean(axis=(1, 3))
    return jnp.broadcast_to(means[:, None, :, None], (height // 4, 4, breadth // 4, 4)).reshape(
        height, breadth
    )


def matmul(left, right):
    return jnp.dot(left, right, preferred_element_type=jnp.float32)


def inner_first(left, right):
    return lax.dot_general(
        left, right, (((0,), (0,)), ((), ())), preferred_element_type=jnp.float32
    )


def inner_last(left, right):
    return lax.dot_general(
        left, right, (((1,), (1,)), ((), ())), preferred_element_type=jnp.float32
    )


def body(
    tokens,
    target,
    gate_weight,
    up_weight,
    down_weight,
    probe_gate,
    probe_up,
    probe_down,
    first_gate,
    first_up,
    first_down,
    second_gate,
    second_up,
    second_down,
):
    whole = lax.all_gather(tokens, "col", axis=0, tiled=True)
    sign_gate = (2 * probe_gate - 1).astype(jnp.bfloat16)
    sign_up = (2 * probe_up - 1).astype(jnp.bfloat16)
    sign_down = (2 * probe_down - 1).astype(jnp.bfloat16)
    width = gate_weight.shape[1]
    matrices = (gate_weight, up_weight, sign_gate, sign_up)
    block = whole
    sums = lax.psum_scatter(
        jnp.concatenate([matmul(block, matrix) for matrix in matrices], axis=1).astype(
            jnp.bfloat16
        ),
        "row",
        scatter_dimension=0,
        tiled=True,
    ).astype(jnp.float32)
    pre_gate = sums[:, :width]
    pre_up = sums[:, width : 2 * width]
    dot_gate = sums[:, 2 * width : 3 * width]
    dot_up = sums[:, 3 * width :]
    act, slope, bend = activation(pre_gate)
    hidden = (act * pre_up).astype(jnp.bfloat16)
    hidden_dot = (slope * dot_gate * pre_up + act * dot_up).astype(jnp.bfloat16)
    both = jnp.concatenate([hidden, hidden_dot], axis=1)
    panel = lax.all_gather(both, "row", axis=0, tiled=True)
    plain = panel[:, :width]
    tangent = panel[:, width:]
    value = matmul(plain, down_weight)
    along = matmul(tangent, down_weight) + matmul(plain, sign_down)
    terms = jnp.concatenate([value, along], axis=1)
    outputs = lax.psum_scatter(
        terms.astype(jnp.bfloat16), "col", scatter_dimension=0, tiled=True
    ).astype(jnp.float32)
    feats_here = down_weight.shape[1]
    resid = outputs[:, :feats_here] - target.astype(jnp.float32)
    errors = jnp.concatenate(
        [resid.astype(jnp.bfloat16), outputs[:, feats_here:].astype(jnp.bfloat16)], axis=1
    )
    err_all = lax.all_gather(errors, "col", axis=0, tiled=True)
    block = err_all
    err = block[:, :feats_here]
    err_dot = block[:, feats_here:]
    plain = inner_last(err, down_weight)
    along = inner_last(err_dot, down_weight) + inner_last(err, sign_down)
    back = lax.psum_scatter(
        jnp.concatenate([plain, along], axis=1).astype(jnp.bfloat16),
        "row",
        scatter_dimension=0,
        tiled=True,
    ).astype(jnp.float32)
    d_hidden = back[:, :width]
    d_hidden_dot = back[:, width:]
    plain = panel[:, :width]
    tangent = panel[:, width:]
    err = err_all[:, :feats_here]
    err_dot = err_all[:, feats_here:]
    grad_down = inner_first(plain, err)
    hess_down = inner_first(tangent, err) + inner_first(plain, err_dot)
    d_gate = (d_hidden * pre_up * slope).astype(jnp.bfloat16)
    d_up = (d_hidden * act).astype(jnp.bfloat16)
    dd_gate = (
        d_hidden_dot * pre_up * slope
        + d_hidden * dot_up * slope
        + d_hidden * pre_up * bend * dot_gate
    ).astype(jnp.bfloat16)
    dd_up = (d_hidden_dot * act + d_hidden * slope * dot_gate).astype(jnp.bfloat16)
    stacked = jnp.concatenate([d_gate, d_up, dd_gate, dd_up], axis=1)
    block = whole
    grads = inner_first(block, lax.all_gather(stacked, "row", axis=0, tiled=True))
    grad_gate = grads[:, :width]
    grad_up = grads[:, width : 2 * width]
    hess_gate = grads[:, 2 * width : 3 * width]
    hess_up = grads[:, 3 * width :]
    curv_gate = block_mean(jnp.abs(sign_gate.astype(jnp.float32) * hess_gate))
    curv_up = block_mean(jnp.abs(sign_up.astype(jnp.float32) * hess_up))
    curv_down = block_mean(jnp.abs(sign_down.astype(jnp.float32) * hess_down))
    local_grad = (
        jnp.sum(grad_gate * grad_gate) + jnp.sum(grad_up * grad_up) + jnp.sum(grad_down * grad_down)
    )
    local_curv = (
        jnp.sum(curv_gate * curv_gate) + jnp.sum(curv_up * curv_up) + jnp.sum(curv_down * curv_down)
    )
    total_grad, total_curv = lax.psum((local_grad, local_curv), ("row", "col"))
    count = 3.0 * D * FF
    rms_grad = jnp.sqrt(total_grad / count + 1e-06)
    rms_curv = jnp.sqrt(total_curv / count + 1e-06)
    fix_first = 1.0 - 0.9**STEP
    fix_second = 1.0 - 0.95**STEP
    firsts = []
    seconds = []
    updates = []
    for grad, curv, first, second in (
        (grad_gate, curv_gate, first_gate, second_gate),
        (grad_up, curv_up, first_up, second_up),
        (grad_down, curv_down, first_down, second_down),
    ):
        new_first = 0.9 * first + 0.1 * (grad / rms_grad)
        scaled = curv / rms_curv
        new_second = 0.95 * second + 0.05 * (scaled * scaled)
        firsts.append(new_first)
        seconds.append(new_second)
        updates.append(new_first / fix_first / (jnp.sqrt(new_second / fix_second) + 1e-08))
    return (
        firsts[0],
        firsts[1],
        firsts[2],
        seconds[0],
        seconds[1],
        seconds[2],
        updates[0],
        updates[1],
        updates[2],
    )


def solution(mesh):
    placed = (
        P("col", "row"),
        P("col", "row"),
        P("row", "col"),
        P("row", "col"),
        P("col", "row"),
        P("row", "col"),
        P("row", "col"),
        P("col", "row"),
        P("row", "col"),
        P("row", "col"),
        P("col", "row"),
        P("row", "col"),
        P("row", "col"),
        P("col", "row"),
    )
    return jax.shard_map(
        body,
        mesh=mesh,
        in_specs=placed,
        out_specs=(
            P("row", "col"),
            P("row", "col"),
            P("col", "row"),
            P("row", "col"),
            P("row", "col"),
            P("col", "row"),
            P("row", "col"),
            P("row", "col"),
            P("col", "row"),
        ),
        check_vma=False,
    )
```

profile of v0, /device:TPU:0, one launch (start us, length us, event | category | flops | bytes accessed | tf_op | source)
XLA Modules:
  0.0 1177.8 jit_solution(6216494550631343769)
XLA Ops:
  7.2 0.7 all-gather.5.cloned.1.call-update
  8.0 54.0 %all-gather.5.cloned.1.call-done = bf16[1024,1024]{1,0:T(8,128)(2,1)} async-done(((bf16[128,1024]{1,0:T(8,128)(2,1)}), bf16[1024,1024]{1,0:T(8,128)(2,1)}) %all-gather.5.cloned.1.call-update) | async-done | bytes 2097168 | tf_op jit(solution)/shard_map/all_gather | solution.py:59
  62.0 4.3 fusion.9
  66.3 1.7 fusion.8
  68.0 1.7 convolution_convert_fusion.4
  69.6 1.7 convolution_convert_fusion.5
  71.3 15.2 %pad_maximum_fusion = bf16[1024,2752]{0,1:T(8,128)(2,1)} fusion(bf16[1024,688]{0,1:T(8,128)(2,1)S(1)} %fusion.9, bf16[1024,688]{0,1:T(8,128)(2,1)S(1)} %fusion.8, bf16[1024,688]{0,1:T(8,128)(2,1)S(1)} %convolution_convert_fusion.4, bf16[1024,688]{0,1:T(8,128)(2,1)S(1)} %convolution_convert_fusion.5), kind=kLoop, calls=%fused_computation.1 | loop fusion | flops 22544384 | bytes 11272192 | tf_op jit(solution)/shard_map/concatenate | solution.py:67
  86.6 52.3 %reduce-scatter.6.cloned.1.call-done = bf16[256,2752]{0,1:T(8,128)(2,1)} async-done(((bf16[1024,2752]{0,1:T(8,128)(2,1)}), bf16[256,2752]{0,1:T(8,128)(2,1)}) %reduce-scatter.6.cloned.1.call-update) | async-done | bytes 1409040 | tf_op jit(solution)/shard_map/reduce_scatter | solution.py:66
  138.9 1.6 convert_element_type.55
  140.5 1.5 copy-done.2
  142.0 0.4 multiply_convert_fusion.2
  142.4 0.9 pad_maximum_fusion.4
  143.3 10.7 reduce-scatter.10.cloned.1.call-start
  154.0 16.5 %all-gather.7.cloned.1.call-done = bf16[1024,1376]{0,1:T(8,128)(2,1)} async-done(((bf16[256,1376]{0,1:T(8,128)(2,1)}), bf16[1024,1376]{0,1:T(8,128)(2,1)}) %all-gather.7.cloned.1.call-update) | async-done | bytes 2818064 | tf_op jit(solution)/shard_map/all_gather | solution.py:82
  170.5 3.3 fusion.17
  173.9 1.8 convolution_convert_fusion
  175.7 1.9 add_convert_fusion
  177.6 2.4 pad_maximum_fusion.1
  180.0 6.5 copy.33
  186.6 0.9 copy-done.22
  187.5 0.2 copy.32
  187.7 87.4 %reduce-scatter.10.cloned.1.call-done = bf16[128,2048]{1,0:T(8,128)(2,1)} async-done(((bf16[1024,2048]{1,0:T(8,128)(2,1)}), bf16[128,2048]{1,0:T(8,128)(2,1)}) %reduce-scatter.10.cloned.1.call-update) | async-done | bytes 524304
  275.1 1.1 fusion.35
  276.1 0.2 copy.36
  276.3 0.2 copy.35
  276.5 0.1 subtract_convert_fusion
  276.6 0.8 pad_maximum_fusion.5
  277.5 74.4 %all-gather.9.cloned.1.call-done = bf16[1024,2048]{0,1:T(8,128)(2,1)} async-done(((bf16[128,2048]{0,1:T(8,128)(2,1)}), bf16[1024,2048]{0,1:T(8,128)(2,1)}) %all-gather.9.cloned.1.call-update) | async-done | bytes 4194320 | tf_op jit(solution)/shard_map/all_gather | solution.py:96
  351.9 3.4 fusion.4
  355.2 1.6 convolution_convert_fusion.1
  356.9 0.1 copy-done.8
  357.0 1.6 add_convert_fusion.1
  358.7 1.8 pad_maximum_fusion.2
  360.6 33.9 %reduce-scatter.8.cloned.1.call-done = bf16[256,1376]{0,1:T(8,128)(2,1)} async-done(((bf16[1024,1376]{0,1:T(8,128)(2,1)}), bf16[256,1376]{0,1:T(8,128)(2,1)}) %reduce-scatter.8.cloned.1.call-update) | async-done | bytes 704528 | tf_op jit(solution)/shard_map/reduce_scatter | solution.py:102
  394.4 1.2 convert_element_type.61
  395.7 0.8 multiply_convert_fusion.1
  396.5 1.2 pad_maximum_fusion.3
  397.7 1.1 copy-done.19
  398.8 3.4 fusion.10
  402.2 0.3 copy-done.17
  402.5 0.8 copy-done.20
  403.3 1.8 multiply_abs_fusion
  405.0 94.8 %reshape.56 = f32[172,4,256,4]{3,2,1,0:T(8,128)} reshape(f32[688,1024]{1,0:T(8,128)S(1)} %multiply_abs_fusion) | data formatting | bytes 5636096 | tf_op jit(solution)/shard_map/reshape | solution.py:21
  499.9 27.6 %reduce_sum.88 = f32[172,256]{1,0:T(8,128)S(1)} reduce(f32[172,4,256,4]{3,2,1,0:T(8,128)} %reshape.56, f32[]{:T(128)} %constant.20.clone.1), dimensions={1,3}, to_apply=%region_11.0 | reduce | flops 660480 | bytes 2994180 | tf_op jit(solution)/shard_map/reduce_sum | solution.py:21
  527.5 2.0 broadcast_reduce_fusion
  529.6 5.4 multiply_reduce_fusion
  535.0 8.9 convolution_bitcast_fusion
  543.9 5.1 fusion
  549.0 95.3 %reshape.55 = f32[256,4,172,4]{1,0,3,2:T(8,128)} reshape(f32[1024,688]{0,1:T(8,128)} %get-tuple-element.25) | data formatting | bytes 5636096 | tf_op jit(solution)/shard_map/reshape | solution.py:21
  644.3 27.6 %reduce_sum.86 = f32[256,172]{0,1:T(8,128)S(1)} reduce(f32[256,4,172,4]{1,0,3,2:T(8,128)} %reshape.55, f32[]{:T(128)} %constant.20.clone.1), dimensions={1,3}, to_apply=%region_9.0 | reduce | flops 660480 | bytes 2994180 | tf_op jit(solution)/shard_map/reduce_sum | solution.py:21
  671.9 94.4 %reshape.54 = f32[256,4,172,4]{1,0,3,2:T(8,128)} reshape(f32[1024,688]{0,1:T(8,128)S(1)} %get-tuple-element.26) | data formatting | bytes 5636096 | tf_op jit(solution)/shard_map/reshape | solution.py:21
  766.3 27.6 %reduce_sum.84 = f32[256,172]{0,1:T(8,128)S(1)} reduce(f32[256,4,172,4]{1,0,3,2:T(8,128)} %reshape.54, f32[]{:T(128)} %constant.20.clone.1), dimensions={1,3}, to_apply=%region_7.0 | reduce | flops 660480 | bytes 2994180 | tf_op jit(solution)/shard_map/reduce_sum | solution.py:21
  795.9 2.1 broadcast_reduce_fusion.1
  799.9 39.5 %all-reduce = (f32[]{:T(128)}, f32[]{:T(128)}) all-reduce(f32[]{:T(128)S(6)} %add.101, f32[]{:T(128)S(6)} %add.108), channel_id=1, replica_groups=mesh['row'=4,'col'=8] {'row','col'}, use_global_device_ids=true, to_apply=%region_6.0 | all-reduce | flops 2 | bytes 16 | tf_op jit(solution)/shard_map/psum | solution.py:140
  840.2 28.4 %broadcast_in_dim.28 = f32[256,4,172,4]{1,0,3,2:T(8,128)} broadcast(f32[256,172]{0,1:T(8,128)S(1)} %multiply_multiply_fusion.1), dimensions={0,2} | broadcast | bytes 2994176 | tf_op jit(solution)/shard_map/broadcast_in_dim | solution.py:22
  868.6 75.0 %mul.241 = f32[1024,688]{0,1:T(8,128)} reshape(f32[256,4,172,4]{1,0,3,2:T(8,128)} %broadcast_in_dim.28) | data formatting | bytes 5636096 | tf_op jit(solution)/shard_map/mul | solution.py:156
  944.3 28.4 %broadcast_in_dim.27 = f32[256,4,172,4]{1,0,3,2:T(8,128)} broadcast(f32[256,172]{0,1:T(8,128)S(1)} %multiply_multiply_fusion.2), dimensions={0,2} | broadcast | bytes 2994176 | tf_op jit(solution)/shard_map/broadcast_in_dim | solution.py:22
  972.7 75.0 %mul.237 = f32[1024,688]{0,1:T(8,128)} reshape(f32[256,4,172,4]{1,0,3,2:T(8,128)} %broadcast_in_dim.27) | data formatting | bytes 5636096 | tf_op jit(solution)/shard_map/mul | solution.py:156
  1047.7 28.3 %broadcast_in_dim.29 = f32[172,4,256,4]{3,2,1,0:T(8,128)} broadcast(f32[172,256]{1,0:T(8,128)S(1)} %multiply_multiply_fusion), dimensions={0,2} | broadcast | bytes 2994176 | tf_op jit(solution)/shard_map/broadcast_in_dim | solution.py:22
  1075.9 74.7 %mul.247 = f32[688,1024]{1,0:T(8,128)S(1)} reshape(f32[172,4,256,4]{3,2,1,0:T(8,128)} %broadcast_in_dim.29) | data formatting | bytes 5636096 | tf_op jit(solution)/shard_map/mul | solution.py:156
  1150.7 8.6 add_divide_fusion
  1159.3 1.0 copy-done.14
  1160.4 0.8 copy-done.15
  1161.2 9.6 add_divide_fusion.1
  (63 shorter events, 0.6 us)
Async XLA Ops:
  7.2 163.3 %copy-start = (bf16[688,1024]{1,0:T(8,128)(2,1)S(1)}, bf16[688,1024]{1,0:T(8,128)(2,1)}, u32[]{:S(2)}) copy-start(bf16[688,1024]{1,0:T(8,128)(2,1)} %param.18) | copy-start | bytes 4227076
  7.2 54.8 %all-gather.5.cloned.1.call-start = ((), (), s32[]{:S(2)}) async-start(), calls=%async_computation.3 | async-start | bytes 2359296 | tf_op jit(solution)/shard_map/all_gather | solution.py:59
  7.9 131.0 %reduce-scatter.6.cloned.1.call-start = ((), (), s32[]{:S(2)}) async-start(), calls=%async_computation.4 | async-start | bytes 7045120 | tf_op jit(solution)/shard_map/reduce_scatter | solution.py:66
  62.0 4.3 copy-start.11
  62.0 4.3 copy-start.23
  66.3 1.7 copy-start.24
  67.9 1.7 copy-start.25
  86.6 83.9 %all-gather.7.cloned.1.call-start = ((), (), s32[]{:S(2)}) async-start(), calls=%async_computation.5 | async-start | bytes 3522560 | tf_op jit(solution)/shard_map/all_gather | solution.py:82
  140.5 1.6 copy-start.2
  143.3 131.7 %reduce-scatter.10.cloned.1.call-start = ((), (), s32[]{:S(2)}) async-start(), calls=%async_computation.9 | async-start | bytes 4718592
  170.5 3.4 copy-start.18
  173.9 1.9 copy-start.7
  186.5 0.9 copy-start.22
  186.6 165.3 %all-gather.9.cloned.1.call-start = ((), (), s32[]{:S(2)}) async-start(), calls=%async_computation.6 | async-start | bytes 4718592 | tf_op jit(solution)/shard_map/all_gather | solution.py:96
  277.4 117.0 %reduce-scatter.8.cloned.1.call-start = ((), (), s32[]{:S(2)}) async-start(), calls=%async_computation.7 | async-start | bytes 3522560 | tf_op jit(solution)/shard_map/reduce_scatter | solution.py:102
  351.9 3.4 copy-start.16
  355.2 1.8 copy-start.8
  360.5 35.1 %copy-start.3 = (f32[256,2752]{0,1:T(8,128)S(1)}, f32[256,2752]{0,1:T(8,128)}, u32[]{:S(2)}) copy-start(f32[256,2752]{0,1:T(8,128)} %copy-done.2) | copy-start | bytes 8454148
  360.5 174.4 %all-gather.11.cloned.1.call-start = ((), (), s32[]{:S(2)}) async-start(), calls=%async_computation.8 | async-start | bytes 7045120 | tf_op jit(solution)/shard_map/all_gather | solution.py:126
  396.5 2.3 copy-start.19
  398.8 3.4 copy-start.9
  398.8 3.7 copy-start.17
  398.8 4.5 copy-start.20
  499.9 29.7 %copy-start.21 = (bf16[1024,1376]{0,1:T(8,128)(2,1)S(1)}, bf16[1024,1376]{0,1:T(8,128)(2,1)}, u32[]{:S(2)}) copy-start(bf16[1024,1376]{0,1:T(8,128)(2,1)} %all-gather.7.cloned.1.call-done) | copy-start | bytes 8454148
  535.0 8.9 copy-start.10
  535.0 8.9 copy-start.12
  543.9 5.1 copy-start.4
  1150.6 8.7 copy-start.5
  1150.6 8.7 copy-start.6
  1150.7 8.7 copy-start.13
  1150.7 9.7 copy-start.14
  1150.7 10.5 copy-start.15
  1161.2 9.6 copy-start.1
Sparse Core Ops, SparseCore 0:
  10.1 51.7 all-gather.4
  86.7 52.1 reduce-scatter.5
  143.5 26.9 all-gather.6
  186.7 88.3 reduce-scatter.9
  277.6 74.2 all-gather.8
  360.7 33.7 reduce-scatter.7
  397.8 43.3 all-gather.10
where the time goes:
time: 1190 us; the launch traced here: 1180 us
  local copies, waits for them, and re-layouts  609 us (51%)
  waiting for transfers between devices  319 us (27%)
  other arithmetic  137 us (12%)
  matrix products  42.4 us (4%)
  blocking collectives  39.5 us (3%)
  between operations  20 us (2%)
    reshape x3, local copies, waits for them, and re-layouts, block_mean(): means = values.reshape(height // 4, 4, breadth // 4, 4).mean(axis=(1, 3))  285 us
    mul x3, local copies, waits for them, and re-layouts, body(): new_second = 0.95 * second + 0.05 * (scaled * scaled)  225 us
    unnamed x8, waiting for transfers between devices  88.2 us
    broadcast_in_dim x3, local copies, waits for them, and re-layouts, block_mean(): jnp.broadcast_to(means[:, None, :, None], (height // 4, 4, breadth // 4, 4))  85.1 us
    reduce_sum x3, other arithmetic, block_mean(): means = values.reshape(height // 4, 4, breadth // 4, 4).mean(axis=(1, 3))  82.9 us
    all_gather x1, waiting for transfers between devices, body(): err_all = lax.all_gather(errors, 'col', axis=0, tiled=True)  74.4 us
    all_gather x1, waiting for transfers between devices, body(): whole = lax.all_gather(tokens, 'col', axis=0, tiled=True)  54 us
    reduce_scatter x1, waiting for transfers between devices, body(): lax.psum_scatter(jnp.concatenate([matmul(block, matrix) for matrix in mat...  52.3 us
  transfers between devices with their start and end apart: 7, of which 6 were waited for; matrix products, arithmetic and copies ran while one was open for 11% of the time, Pallas kernels for 0%

commit v1 on v0

v1 whole, which is shorter than its diff:
```python
import jax
import jax.numpy as jnp
from jax import lax
from jax.experimental import pallas as pl
from jax.experimental.pallas import tpu as pltpu
from jax.sharding import PartitionSpec as P


STEP = 10
BF = jnp.bfloat16
F32 = jnp.float32


def dot(left, right, inner):
    return lax.dot_general(left, right, (((inner[0],), (inner[1],)), ((), ())), preferred_element_type=F32)


def pick(blocks, index):
    chosen = blocks[0]
    for at in range(1, len(blocks)):
        chosen = jnp.where(index == at, blocks[at], chosen)
    return chosen


def pair_swap(value, axis, size):
    return lax.ppermute(value, axis, [(i, i ^ 1) for i in range(size)])


def ring_up(value, axis, size):
    return lax.ppermute(value, axis, [(i, (i + 2) % size) for i in range(size)])


def total_over_all(value, sizes):
    for axis, size in sizes:
        step = 1
        while step < size:
            if size % (2 * step) == 0:
                value = value + lax.ppermute(value, axis, [(i, i ^ step) for i in range(size)])
                step *= 2
            else:
                raise ValueError("axis size")
    return value


def sign_kernel(gate_ref, up_ref, down_ref, sign_gate_ref, sign_up_ref, sign_down_ref):
    for probe, sign in ((gate_ref, sign_gate_ref), (up_ref, sign_up_ref), (down_ref, sign_down_ref)):
        sign[...] = (2 * probe[...] - 1).astype(F32).astype(BF)


def side(feats):
    return 256 if feats % 256 == 0 else 128


def cols_tile(rows, tile):
    return pl.BlockSpec((rows, tile), lambda i: (0, i))


def fixed(shape):
    return pl.BlockSpec(shape, lambda i: (0, 0))


def signs(*probes):
    width, feats = probes[0].shape
    tile = side(feats)
    specs = [cols_tile(width, tile)] * 3
    return pl.pallas_call(
        sign_kernel,
        grid=(feats // tile,),
        in_specs=specs,
        out_specs=specs,
        out_shape=[jax.ShapeDtypeStruct(p.shape, BF) for p in probes],
        name="signs",
    )(*probes)


def same_block():
    down = lax.broadcasted_iota(jnp.int32, (256, 256), 0) >> 2
    across = lax.broadcasted_iota(jnp.int32, (256, 256), 1) >> 2
    return jnp.where(down == across, 1.0, 0.0).astype(BF)


def finish_weight(grad, hess, sign, grad_ref, curv_ref, grad_sum, curv_sum):
    height, breadth = hess.shape
    grad_ref[...] = grad
    grad_sum[...] += jnp.sum(grad * grad, axis=0, keepdims=True)
    same = same_block()
    size = jnp.abs(sign.astype(F32) * hess).astype(BF)
    total = curv_sum[...]
    for top in range(0, height, 256):
        tall = min(256, height - top)
        sums = jnp.dot(same[:tall, :tall], size[top : top + tall], preferred_element_type=F32)
        means = jnp.dot(
            (sums * 0.0625).astype(BF), same[:breadth, :breadth], preferred_element_type=F32
        )
        curv_ref[top : top + tall, :] = means
        total = total + jnp.sum(means * means, axis=0, keepdims=True)
    curv_sum[...] = total


def pack_sums(grad_sum, curv_sum):
    lane = lax.broadcasted_iota(jnp.int32, (8, 128), 1)
    first = jnp.where(lane == 0, jnp.sum(grad_sum[...]), 0.0)
    return jnp.where(lane == 1, jnp.sum(curv_sum[...]), first)


def in_order(core, refs):
    shards = []
    for current, other in zip(refs[::2], refs[1::2]):
        one = current[...]
        two = other[...]
        shards += [jnp.where(core == 0, one, two), jnp.where(core == 0, two, one)]
    return jnp.concatenate(shards, axis=0)


def down_kernel(pieces, *refs):
    core_ref, panel_ref, sign_ref = refs[:3]
    err_refs = refs[3 : 3 + pieces]
    dot_refs = refs[3 + pieces : 3 + 2 * pieces]
    grad_ref, curv_ref, pack_ref, grad_sum, curv_sum = refs[3 + 2 * pieces :]

    @pl.when(pl.program_id(0) == 0)
    def _():
        grad_sum[...] = jnp.zeros_like(grad_sum)
        curv_sum[...] = jnp.zeros_like(curv_sum)

    width = sign_ref.shape[0]
    err = in_order(core_ref[0], err_refs)
    err_dot = in_order(core_ref[0], dot_refs)
    plain = panel_ref[:width, :]
    grad = jnp.dot(plain, err, preferred_element_type=F32)
    hess = jnp.dot(panel_ref[width:, :], err, preferred_element_type=F32)
    hess = hess + jnp.dot(plain, err_dot, preferred_element_type=F32)
    finish_weight(grad, hess, sign_ref[...], grad_ref, curv_ref, grad_sum, curv_sum)

    @pl.when(pl.program_id(0) == pl.num_programs(0) - 1)
    def _():
        pack_ref[...] = pack_sums(grad_sum, curv_sum)


def down_grads(core, panel, sign, errs, dots):
    width, feats = sign.shape
    tile = side(feats)
    each = [cols_tile(errs[0].shape[0], tile)] * len(errs)
    return pl.pallas_call(
        lambda *refs: down_kernel(len(errs), *refs),
        grid=(feats // tile,),
        in_specs=[
            pl.BlockSpec(memory_space=pltpu.SMEM), fixed(panel.shape), cols_tile(width, tile), *each, *each
        ],
        out_specs=[cols_tile(width, tile), cols_tile(width, tile), fixed((8, 128))],
        out_shape=[
            jax.ShapeDtypeStruct((width, feats), F32),
            jax.ShapeDtypeStruct((width, feats), F32),
            jax.ShapeDtypeStruct((8, 128), F32),
        ],
        scratch_shapes=[pltpu.VMEM((1, tile), F32), pltpu.VMEM((1, tile), F32)],
        compiler_params=pltpu.CompilerParams(dimension_semantics=("arbitrary",)),
        cost_estimate=pl.CostEstimate(
            flops=6 * width * feats * panel.shape[1], transcendentals=0, bytes_accessed=12 * width * feats
        ),
        name="down_grads",
    )(core, panel, sign, *errs, *dots)


def wide_kernel(pieces, *refs):
    core_ref, sign_gate_ref, sign_up_ref, before_ref, cot_ref = refs[:5]
    token_refs = refs[5 : 5 + pieces]
    grad_gate_ref, curv_gate_ref, grad_up_ref, curv_up_ref, pack_ref, grad_sum, curv_sum = refs[5 + pieces :]

    @pl.when(pl.program_id(0) == 0)
    def _():
        grad_sum[...] = jnp.zeros_like(grad_sum)
        curv_sum[...] = jnp.zeros_like(curv_sum)

    width = sign_gate_ref.shape[0]
    tokens = in_order(core_ref[0], token_refs)

    def product(at):
        return jnp.dot(cot_ref[at * width : (at + 1) * width, :], tokens, preferred_element_type=F32)

    finish_weight(
        product(0), product(2), sign_gate_ref[...], grad_gate_ref, curv_gate_ref, grad_sum, curv_sum
    )
    finish_weight(product(1), product(3), sign_up_ref[...], grad_up_ref, curv_up_ref, grad_sum, curv_sum)

    @pl.when(pl.program_id(0) == pl.num_programs(0) - 1)
    def _():
        pack_ref[...] = before_ref[...] + pack_sums(grad_sum, curv_sum)


def wide_grads(core, sign_gate, sign_up, before, cots, tokens):
    width, feats = sign_gate.shape
    tile = side(feats)
    out = cols_tile(width, tile)
    count = cots.shape[1]
    return pl.pallas_call(
        lambda *refs: wide_kernel(len(tokens), *refs),
        grid=(feats // tile,),
        in_specs=[
            pl.BlockSpec(memory_space=pltpu.SMEM), out, out, fixed((8, 128)), fixed(cots.shape),
            *[cols_tile(t.shape[0], tile) for t in tokens],
        ],
        out_specs=[out, out, out, out, fixed((8, 128))],
        out_shape=[jax.ShapeDtypeStruct((width, feats), F32)] * 4 + [jax.ShapeDtypeStruct((8, 128), F32)],
        scratch_shapes=[pltpu.VMEM((1, tile), F32), pltpu.VMEM((1, tile), F32)],
        compiler_params=pltpu.CompilerParams(dimension_semantics=("arbitrary",)),
        cost_estimate=pl.CostEstimate(
            flops=8 * width * feats * count, transcendentals=0, bytes_accessed=20 * width * feats
        ),
        name="wide_grads",
    )(core, sign_gate, sign_up, before, cots, *tokens)


def cotangent_kernel(keep_ref, send_ref, by_keep_ref, by_send_ref, *refs):
    out_ref = refs[-1]
    width = keep_ref.shape[0] // 2
    count = keep_ref.shape[1]
    for at, (d_ref, by_ref) in enumerate(((keep_ref, by_keep_ref), (send_ref, by_send_ref))):
        lanes = slice(at * count, (at + 1) * count)
        d_hidden = d_ref[:width].astype(F32)
        d_hidden_dot = d_ref[width:].astype(F32)
        for_gate = by_ref[:width].astype(F32)
        for_up = by_ref[width : 2 * width].astype(F32)
        out_ref[:width, lanes] = (d_hidden * for_gate).astype(BF)
        out_ref[width : 2 * width, lanes] = (d_hidden * for_up).astype(BF)
        out_ref[2 * width : 3 * width, lanes] = (
            d_hidden_dot * for_gate + d_hidden * by_ref[2 * width : 3 * width].astype(F32)
        ).astype(BF)
        out_ref[3 * width :, lanes] = (
            d_hidden_dot * for_up + d_hidden * by_ref[3 * width :].astype(F32)
        ).astype(BF)


def cotangents_of(at, pieces, panel, *args):
    height = args[2].shape[0]
    wide = 2 * args[0].shape[1]
    more = [] if panel is None else [panel]
    return pl.pallas_call(
        cotangent_kernel,
        grid=(1,),
        in_specs=[fixed(v.shape) for v in args] + [pl.BlockSpec(memory_space=pl.ANY)] * len(more),
        out_specs=pl.BlockSpec((height, wide), lambda i: (0, at)),
        out_shape=jax.ShapeDtypeStruct((height, wide * pieces), BF),
        input_output_aliases={4: 0} if more else {},
        cost_estimate=pl.CostEstimate(
            flops=4 * height * wide, transcendentals=0, bytes_accessed=6 * height * wide
        ),
        name="cotangents",
    )(*args, *more)


def update_kernel(scale_ref, *refs):
    fix_first = 1.0 - 0.9**STEP
    fix_second = 1.0 - 0.95**STEP
    by_grad = scale_ref[0]
    by_curv = scale_ref[1]
    for at in range(3):
        grad, curv, first, second = (refs[4 * at + n][...] for n in range(4))
        first_ref, second_ref, update_ref = (refs[12 + 3 * n + at] for n in range(3))
        new_first = 0.9 * first + 0.1 * (grad * by_grad)
        scaled = curv * by_curv
        new_second = 0.95 * second + 0.05 * (scaled * scaled)
        first_ref[...] = new_first
        second_ref[...] = new_second
        update_ref[...] = new_first * (1.0 / fix_first) / (jnp.sqrt(new_second * (1.0 / fix_second)) + 1e-08)


def update(scales, weights):
    width, feats = weights[0][0].shape
    tall = cols_tile(width, 128)
    shapes = [jax.ShapeDtypeStruct(w[0].shape, F32) for w in weights]
    return pl.pallas_call(
        update_kernel,
        grid=(feats // 128,),
        in_specs=[pl.BlockSpec(memory_space=pltpu.SMEM)] + [tall] * 12,
        out_specs=[tall] * 9,
        out_shape=shapes * 3,
        name="update",
    )(scales, *weights[0], *weights[1], *weights[2])


def activation(pre):
    sig = jax.nn.sigmoid(pre)
    act = pre * sig
    slope = sig * (1.0 + pre * (1.0 - sig))
    bend = sig * (1.0 - sig) * (2.0 + pre * (1.0 - 2.0 * sig))
    return (act, slope, bend)


def make_body(n_row, n_col):
    outer = n_row // 2
    rings = n_col // 2
    groups = rings // outer
    if n_row % 2 or n_col % 2 or rings % outer:
        raise ValueError("mesh")

    def body(
        tokens, target, gate_weight, up_weight, down_weight, probe_gate, probe_up, probe_down,
        first_gate, first_up, first_down, second_gate, second_up, second_down,
    ):
        row = lax.axis_index("row")
        core = row % 2
        chip = row // 2
        core_line = jnp.reshape(core, (1,)).astype(jnp.int32)
        gate_weight, up_weight, probe_gate, probe_up, first_gate, first_up, second_gate, second_up = (
            v.T
            for v in (
                gate_weight, up_weight, probe_gate, probe_up, first_gate, first_up, second_gate, second_up
            )
        )
        width, feats = gate_weight.shape
        count = tokens.shape[0]
        sign_gate, sign_up, sign_down = signs(probe_gate, probe_up, probe_down)

        token_pieces = []
        pre_keeps = []
        current = tokens
        for k in range(rings):
            other = pair_swap(current, "col", n_col)
            following = ring_up(current, "col", n_col) if k < rings - 1 else None
            keep = jnp.where(core == 0, current, other)
            send = jnp.where(core == 0, other, current)
            piece = jnp.concatenate([keep, send], axis=0)
            token_pieces += [current, other]
            current = following
            parts = [dot(matrix, piece, (1, 1)) for matrix in (gate_weight, up_weight, sign_gate, sign_up)]
            sent = jnp.concatenate([part[:, count:].astype(BF) for part in parts], axis=0)
            kept = jnp.concatenate([part[:, :count] for part in parts], axis=0)
            pre_keeps.append(kept + pair_swap(sent, "row", n_row).astype(F32))

        hidden_keeps = []
        hidden_sends = []
        owned = []
        for g in range(groups):
            mine = pre_keeps[g * outer : (g + 1) * outer]
            current = pick(mine, (chip - 1) % outer)
            for s in range(1, outer):
                got = ring_up(current.astype(BF), "row", n_row)
                current = got.astype(F32) + pick(mine, (chip - s - 1) % outer)
            pre_gate = current[:width]
            pre_up = current[width : 2 * width]
            dot_gate = current[2 * width : 3 * width]
            dot_up = current[3 * width :]
            act, slope, bend = activation(pre_gate)
            owned.append(
                jnp.concatenate(
                    [
                        (pre_up * slope).astype(BF),
                        act.astype(BF),
                        (dot_up * slope + pre_up * bend * dot_gate).astype(BF),
                        (slope * dot_gate).astype(BF),
                    ],
                    axis=0,
                )
            )
            hidden = (act * pre_up).astype(BF)
            hidden_dot = (slope * dot_gate * pre_up + act * dot_up).astype(BF)
            keeps = by_owner(gather_blocks(jnp.concatenate([hidden, hidden_dot], axis=0)), chip)
            both = jnp.concatenate(keeps, axis=1)
            sends = pair_swap(both, "row", n_row)
            hidden_keeps.append(both)
            hidden_sends.append(sends)

        near = ([], [])
        far = ([], [])
        for g in range(groups):
            sides = []
            for panel in (hidden_keeps[g], hidden_sends[g]):
                value = dot(panel[:width], down_weight, (0, 0))
                along = dot(panel[width:], down_weight, (0, 0)) + dot(panel[:width], sign_down, (0, 0))
                sides.append((value, along))
            for j in range(outer):
                for part in range(2):
                    own = sides[0][part][j * count : (j + 1) * count]
                    alien = sides[1][part][j * count : (j + 1) * count]
                    near[part].append(jnp.where(core == 0, own, alien))
                    far[part].append(jnp.where(core == 0, alien, own).astype(BF))
        order = [*range(1, rings), 0]
        reduced = {}
        for k in order:
            for part in range(2):
                reduced[k, part] = near[part][k] + pair_swap(far[part][k], "col", n_col).astype(F32)
        outputs = [reduced[order[0], part] for part in range(2)]
        for k in order[1:]:
            for part in range(2):
                moved = ring_up(outputs[part].astype(BF), "col", n_col)
                outputs[part] = moved.astype(F32) + reduced[k, part]
        errors = [(outputs[0] - target.astype(F32)).astype(BF), outputs[1].astype(BF)]

        pre_parts = []
        for g in range(groups):
            got = gather_blocks(owned[g])
            errors[0], *got = lax.optimization_barrier((errors[0], *got))
            keeps = by_owner(got, chip)
            for j in range(outer):
                pre_parts.append((keeps[j], pair_swap(keeps[j], "row", n_row)))

        error_pieces = ([], [])
        error_shards = ([], [])
        cots = None
        for k in range(rings):
            for part in range(2):
                current = errors[part]
                other = pair_swap(current, "col", n_col)
                if k < rings - 1:
                    errors[part] = ring_up(current, "col", n_col)
                keep = jnp.where(core == 0, current, other)
                send = jnp.where(core == 0, other, current)
                error_shards[part].extend([current, other])
                error_pieces[part].append(jnp.concatenate([keep, send], axis=0))
            err, err_dot = error_pieces[0][k], error_pieces[1][k]
            plain = dot(down_weight, err, (1, 1))
            along = dot(down_weight, err_dot, (1, 1)) + dot(sign_down, err, (1, 1))
            sent = jnp.concatenate([plain[:, count:].astype(BF), along[:, count:].astype(BF)], axis=0)
            kept = jnp.concatenate([plain[:, :count], along[:, :count]], axis=0)
            total = kept + pair_swap(sent, "row", n_row).astype(F32)
            moving = total.astype(BF)
            for _ in range(1, outer):
                moving = ring_up(moving, "row", n_row)
                total = total + moving.astype(F32)
            keep_d = total.astype(BF)
            send_d = pair_swap(keep_d, "row", n_row)
            cots = cotangents_of(k, rings, cots, keep_d, send_d, *pre_parts[k])

        lanes = []
        for g in range(groups):
            for j in range(outer):
                lanes.append(hidden_keeps[g][:, j * count : (j + 1) * count])
                lanes.append(hidden_sends[g][:, j * count : (j + 1) * count])
        panel = jnp.concatenate(lanes, axis=1)
        grad_down, curv_down, partial = down_grads(core_line, panel, sign_down, *error_shards)
        grad_gate, curv_gate, grad_up, curv_up, packed = wide_grads(
            core_line, sign_gate, sign_up, partial, cots, token_pieces
        )
        packed = total_over_all(packed, (("row", n_row), ("col", n_col)))
        entries = 3.0 * feats * n_row * width * n_col
        scales = 1.0 / jnp.sqrt(packed[0, :2] / entries + 1e-06)
        results = update(
            scales,
            (
                (grad_gate, curv_gate, first_gate, second_gate),
                (grad_up, curv_up, first_up, second_up),
                (grad_down, curv_down, first_down, second_down),
            ),
        )
        return tuple(v if i % 3 == 2 else v.T for i, v in enumerate(results))

    def gather_blocks(block):
        got = [block]
        for _ in range(1, outer):
            got.append(ring_up(got[-1], "row", n_row))
        return got

    def by_owner(got, chip):
        return [pick(got, (chip - j) % outer) for j in range(outer)]

    return body


def solution(mesh):
    wide = P("row", "col")
    tall = P("col", "row")
    inner = make_body(mesh.shape["row"], mesh.shape["col"])

    return jax.shard_map(
        inner,
        mesh=mesh,
        in_specs=(tall, tall, wide, wide, tall, wide, wide, tall, wide, wide, tall, wide, wide, tall),
        out_specs=(wide, wide, tall, wide, wide, tall, wide, wide, tall),
        check_vma=False,
    )
```

time: 1190 us -> 387 us (0.33)
  local copies, waits for them, and re-layouts: 609 us -> 8.84 us
  other arithmetic: 137 us -> 8.35 us
  waiting for transfers between devices: 319 us -> 227 us
  Pallas kernels: 0 us -> 66.4 us
  blocking collectives: 39.5 us -> 0 us
  starting transfers between devices: 10.9 us -> 44.7 us
  matrix products: 42.4 us -> 24.8 us
  between operations: 20 us -> 2.45 us
    reshape x3 -> x0, local copies, waits for them, and re-layouts: 285 us -> none  [block_mean(): means = values.reshape(height // 4, 4, breadth // 4, 4).mean(axis=(1, 3))]
    ppermute x0 -> x68, waiting for transfers between devices: none -> 227 us  [the longest x25 136 us: ring_up(): return lax.ppermute(value, axis, [(i, (i + 2) % size) for i in range(size)])]
    mul x3 -> x0, local copies, waits for them, and re-layouts: 225 us -> none  [body(): new_second = 0.95 * second + 0.05 * (scaled * scaled)]
    all_gather x4 -> x0, waiting for transfers between devices: 145 us -> none  [the longest x1 74.4 us: body(): err_all = lax.all_gather(errors, 'col', axis=0, tiled=True)]
    unnamed x8 -> x0, waiting for transfers between devices: 88.2 us -> none
    reduce_sum x5 -> x0, other arithmetic: 87 us -> none  [the longest x3 82.9 us: block_mean(): means = values.reshape(height // 4, 4, breadth // 4, 4).mean(axis=(1, 3))]
    reduce_scatter x2 -> x0, waiting for transfers between devices: 86.1 us -> none  [the longest x1 52.3 us: body(): lax.psum_scatter(jnp.concatenate([matmul(block, matrix) for matrix in mat...]
    broadcast_in_dim x3 -> x0, local copies, waits for them, and re-layouts: 85.1 us -> none  [block_mean(): jnp.broadcast_to(means[:, None, :, None], (height // 4, 4, breadth // 4, 4))]
  transfers between devices with their start and end apart: 7 -> 68, of which waited for: 6 -> 40; matrix products, arithmetic and copies ran while one was open for 11% -> 9% of each run, Pallas kernels for 0% -> 7%
where the time goes in v1:
time: 387 us; the launch traced here: 382 us
  waiting for transfers between devices  227 us (59%)
  Pallas kernels  66.4 us (17%)
  starting transfers between devices  44.7 us (12%)
  matrix products  24.8 us (6%)
  local copies, waits for them, and re-layouts  8.84 us (2%)
  other arithmetic  8.35 us (2%)
    ppermute x25, waiting for transfers between devices, ring_up(): return lax.ppermute(value, axis, [(i, (i + 2) % size) for i in range(size)])  136 us
    ppermute x38, waiting for transfers between devices, pair_swap(): return lax.ppermute(value, axis, [(i, i ^ 1) for i in range(size)])  76.1 us
    dot_general x40, matrix products, dot(): lax.dot_general(left, right, (((inner[0],), (inner[1],)), ((), ())), pref...  24.8 us
    ppermute x38, starting transfers between devices, pair_swap(): return lax.ppermute(value, axis, [(i, i ^ 1) for i in range(size)])  24.4 us
    pallas_call x1, Pallas kernels, update(): pl.pallas_call(update_kernel, grid=(feats // 128,), in_specs=[pl.BlockSpe...  21.7 us
    ppermute x25, starting transfers between devices, ring_up(): return lax.ppermute(value, axis, [(i, (i + 2) % size) for i in range(size)])  17.6 us
    pallas_call x1, Pallas kernels, wide_grads(): pl.pallas_call(lambda *refs: wide_kernel(len(tokens), *refs), grid=(feats...  14.3 us
    ppermute x5, waiting for transfers between devices, total_over_all(): lax.ppermute(value, axis, [(i, i ^ step) for i in range(size)])  14.1 us
  transfers between devices with their start and end apart: 68, of which 40 were waited for; matrix products, arithmetic and copies ran while one was open for 9% of the time, Pallas kernels for 7%

profile of v1, /device:TPU:0, one launch (start us, length us, event | category | flops | bytes accessed | tf_op | source)
XLA Modules:
  0.0 382.0 jit_solution(8116351411052276694)
XLA Ops:
  0.7 3.1 collective-permute-start.3
  3.7 1.6 collective-permute-start
  5.3 5.7 %signs.1 = (bf16[688,1024]{1,0:T(8,128)(2,1)}, bf16[688,1024]{1,0:T(8,128)(2,1)}, bf16[688,1024]{1,0:T(8,128)(2,1)}) custom-call(s32[688,1024]{1,0:T(8,128)} %bitcast.95, s32[688,1024]{1,0:T(8,128)} %bitcast.96, s32[688,1024]{1,0:T(8,128)} %down_ref.1), custom_call_target="tpu_custom_call" | custom-call | tf_op jit(solution)/shard_map/signs/pallas_call | solution.py:66
  11.1 2.0 convolution_bitcast_fusion.12
  17.7 1.6 collective-permute-start.8
  19.4 4.8 %collective-permute-done.1.refs_8_ = bf16[128,1024]{1,0:T(8,128)(2,1)S(1)} collective-permute-done((bf16[128,1024]{1,0:T(8,128)(2,1)S(1)}, bf16[128,1024]{1,0:T(8,128)(2,1)S(1)}, u32[]{:S(2)}, u32[]{:S(2)}) %collective-permute-start.1) | collective-permute-done | bytes 262176 | tf_op jit(solution)/shard_map/ppermute | solution.py:26
  26.9 1.4 collective-permute-done.8.refs_9_
  30.0 6.2 %collective-permute-done.12.refs_10_ = bf16[128,1024]{1,0:T(8,128)(2,1)S(1)} collective-permute-done((bf16[128,1024]{1,0:T(8,128)(2,1)S(1)}, bf16[128,1024]{1,0:T(8,128)(2,1)S(1)}, u32[]{:S(2)}, u32[]{:S(2)}) %collective-permute-start.12) | collective-permute-done | bytes 262176 | tf_op jit(solution)/shard_map/ppermute | solution.py:26
  38.9 1.5 collective-permute-done.9.refs_11_
  41.6 6.7 %collective-permute-done.10.refs_12_ = bf16[128,1024]{1,0:T(8,128)(2,1)S(1)} collective-permute-done((bf16[128,1024]{1,0:T(8,128)(2,1)S(1)}, bf16[128,1024]{1,0:T(8,128)(2,1)S(1)}, u32[]{:S(2)}, u32[]{:S(2)}) %collective-permute-start.10) | collective-permute-done | bytes 262176 | tf_op jit(solution)/shard_map/ppermute | solution.py:26
  52.0 1.6 collective-permute-start.5
  54.1 1.6 collective-permute-start.14
  55.7 15.0 %collective-permute-done.5 = bf16[2752,128]{1,0:T(8,128)(2,1)S(1)} collective-permute-done((bf16[2752,128]{1,0:T(8,128)(2,1)S(1)}, bf16[2752,128]{1,0:T(8,128)(2,1)S(1)}, u32[]{:S(2)}, u32[]{:S(2)}) %collective-permute-start.5) | collective-permute-done | bytes 704544 | tf_op jit(solution)/shard_map/ppermute | solution.py:30
  71.5 1.6 collective-permute-start.6
  73.7 19.6 %collective-permute-done.6 = bf16[1376,128]{1,0:T(8,128)(2,1)S(1)} collective-permute-done((bf16[1376,128]{1,0:T(8,128)(2,1)S(1)}, bf16[1376,128]{1,0:T(8,128)(2,1)S(1)}, u32[]{:S(2)}, u32[]{:S(2)}) %collective-permute-start.6) | collective-permute-done | bytes 352288 | tf_op jit(solution)/shard_map/ppermute | solution.py:30
  96.9 1.6 collective-permute-start.15
  99.5 16.5 %collective-permute-done.15 = bf16[1376,128]{1,0:T(8,128)(2,1)S(1)} collective-permute-done((bf16[1376,128]{1,0:T(8,128)(2,1)S(1)}, bf16[1376,128]{1,0:T(8,128)(2,1)S(1)}, u32[]{:S(2)}, u32[]{:S(2)}) %collective-permute-start.15) | collective-permute-done | bytes 352288 | tf_op jit(solution)/shard_map/ppermute | solution.py:30
  122.5 5.1 %collective-permute-done.17 = bf16[128,1024]{1,0:T(8,128)(2,1)S(1)} collective-permute-done((bf16[128,1024]{1,0:T(8,128)(2,1)S(1)}, bf16[128,1024]{1,0:T(8,128)(2,1)S(1)}, u32[]{:S(2)}, u32[]{:S(2)}) %collective-permute-start.17) | collective-permute-done | bytes 262176 | tf_op jit(solution)/shard_map/ppermute | solution.py:26
  128.7 9.6 %collective-permute-done.33 = bf16[128,1024]{1,0:T(8,128)(2,1)S(1)} collective-permute-done((bf16[128,1024]{1,0:T(8,128)(2,1)S(1)}, bf16[128,1024]{1,0:T(8,128)(2,1)S(1)}, u32[]{:S(2)}, u32[]{:S(2)}) %collective-permute-start.33) | collective-permute-done | bytes 262176 | tf_op jit(solution)/shard_map/ppermute | solution.py:26
  142.8 5.1 %collective-permute-done.18 = bf16[128,1024]{1,0:T(8,128)(2,1)S(1)} collective-permute-done((bf16[128,1024]{1,0:T(8,128)(2,1)S(1)}, bf16[128,1024]{1,0:T(8,128)(2,1)S(1)}, u32[]{:S(2)}, u32[]{:S(2)}) %collective-permute-start.18) | collective-permute-done | bytes 262176 | tf_op jit(solution)/shard_map/ppermute | solution.py:30
  149.1 7.7 %collective-permute-done.34 = bf16[128,1024]{1,0:T(8,128)(2,1)S(1)} collective-permute-done((bf16[128,1024]{1,0:T(8,128)(2,1)S(1)}, bf16[128,1024]{1,0:T(8,128)(2,1)S(1)}, u32[]{:S(2)}, u32[]{:S(2)}) %collective-permute-start.34) | collective-permute-done | bytes 262176 | tf_op jit(solution)/shard_map/ppermute | solution.py:30
  157.9 5.9 %collective-permute-done.21 = bf16[128,1024]{1,0:T(8,128)(2,1)S(1)} collective-permute-done((bf16[128,1024]{1,0:T(8,128)(2,1)S(1)}, bf16[128,1024]{1,0:T(8,128)(2,1)S(1)}, u32[]{:S(2)}, u32[]{:S(2)}) %collective-permute-start.21) | collective-permute-done | bytes 262176 | tf_op jit(solution)/shard_map/ppermute | solution.py:26
  164.7 1.2 collective-permute-done.20
  166.0 5.6 %collective-permute-done.37 = bf16[128,1024]{1,0:T(8,128)(2,1)S(1)} collective-permute-done((bf16[128,1024]{1,0:T(8,128)(2,1)S(1)}, bf16[128,1024]{1,0:T(8,128)(2,1)S(1)}, u32[]{:S(2)}, u32[]{:S(2)}) %collective-permute-start.37) | collective-permute-done | bytes 262176 | tf_op jit(solution)/shard_map/ppermute | solution.py:26
  172.6 1.7 collective-permute-done.36
  174.6 9.1 %collective-permute-done.22 = bf16[128,1024]{1,0:T(8,128)(2,1)S(1)} collective-permute-done((bf16[128,1024]{1,0:T(8,128)(2,1)S(1)}, bf16[128,1024]{1,0:T(8,128)(2,1)S(1)}, u32[]{:S(2)}, u32[]{:S(2)}) %collective-permute-start.22) | collective-permute-done | bytes 262176 | tf_op jit(solution)/shard_map/ppermute | solution.py:30
  183.9 1.1 collective-permute-start.26
  185.0 4.2 %collective-permute-done.38 = bf16[128,1024]{1,0:T(8,128)(2,1)S(1)} collective-permute-done((bf16[128,1024]{1,0:T(8,128)(2,1)S(1)}, bf16[128,1024]{1,0:T(8,128)(2,1)S(1)}, u32[]{:S(2)}, u32[]{:S(2)}) %collective-permute-start.38) | collective-permute-done | bytes 262176 | tf_op jit(solution)/shard_map/ppermute | solution.py:30
  189.5 1.1 collective-permute-start.40
  193.1 2.8 collective-permute-done.40.refs_12_
  196.6 1.1 collective-permute-start.28
  198.7 6.6 %collective-permute-done.28.refs_6_ = bf16[128,1024]{1,0:T(8,128)(2,1)S(1)} collective-permute-done((bf16[128,1024]{1,0:T(8,128)(2,1)S(1)}, bf16[128,1024]{1,0:T(8,128)(2,1)S(1)}, u32[]{:S(2)}, u32[]{:S(2)}) %collective-permute-start.28) | collective-permute-done | bytes 262176 | tf_op jit(solution)/shard_map/ppermute | solution.py:26
  207.1 6.2 %collective-permute-done.42.refs_14_ = bf16[128,1024]{1,0:T(8,128)(2,1)S(1)} collective-permute-done((bf16[128,1024]{1,0:T(8,128)(2,1)S(1)}, bf16[128,1024]{1,0:T(8,128)(2,1)S(1)}, u32[]{:S(2)}, u32[]{:S(2)}) %collective-permute-start.42) | collective-permute-done | bytes 262176 | tf_op jit(solution)/shard_map/ppermute | solution.py:26
  215.3 6.9 %collective-permute-done.29.refs_7_ = bf16[128,1024]{1,0:T(8,128)(2,1)S(1)} collective-permute-done((bf16[128,1024]{1,0:T(8,128)(2,1)S(1)}, bf16[128,1024]{1,0:T(8,128)(2,1)S(1)}, u32[]{:S(2)}, u32[]{:S(2)}) %collective-permute-start.29) | collective-permute-done | bytes 262176 | tf_op jit(solution)/shard_map/ppermute | solution.py:30
  222.2 1.1 collective-permute-start.30
  223.4 6.9 %collective-permute-done.43.refs_15_ = bf16[128,1024]{1,0:T(8,128)(2,1)S(1)} collective-permute-done((bf16[128,1024]{1,0:T(8,128)(2,1)S(1)}, bf16[128,1024]{1,0:T(8,128)(2,1)S(1)}, u32[]{:S(2)}, u32[]{:S(2)}) %collective-permute-start.43) | collective-permute-done | bytes 262176 | tf_op jit(solution)/shard_map/ppermute | solution.py:30
  230.4 1.1 collective-permute-start.44
  232.1 7.0 %collective-permute-done.44.refs_16_ = bf16[128,1024]{1,0:T(8,128)(2,1)S(1)} collective-permute-done((bf16[128,1024]{1,0:T(8,128)(2,1)S(1)}, bf16[128,1024]{1,0:T(8,128)(2,1)S(1)}, u32[]{:S(2)}, u32[]{:S(2)}) %collective-permute-start.44) | collective-permute-done | bytes 262176 | tf_op jit(solution)/shard_map/ppermute | solution.py:26
  240.6 1.6 collective-permute-start.60
  242.2 6.5 %collective-permute-done.31.refs_9_ = bf16[128,1024]{1,0:T(8,128)(2,1)S(1)} collective-permute-done((bf16[128,1024]{1,0:T(8,128)(2,1)S(1)}, bf16[128,1024]{1,0:T(8,128)(2,1)S(1)}, u32[]{:S(2)}, u32[]{:S(2)}) %collective-permute-start.31) | collective-permute-done | bytes 262176 | tf_op jit(solution)/shard_map/ppermute | solution.py:30
  248.9 1.5 collective-permute-done.60
  251.6 6.0 %collective-permute-done.45.refs_17_ = bf16[128,1024]{1,0:T(8,128)(2,1)S(1)} collective-permute-done((bf16[128,1024]{1,0:T(8,128)(2,1)S(1)}, bf16[128,1024]{1,0:T(8,128)(2,1)S(1)}, u32[]{:S(2)}, u32[]{:S(2)}) %collective-permute-start.45) | collective-permute-done | bytes 262176 | tf_op jit(solution)/shard_map/ppermute | solution.py:30
  257.6 1.1 collective-permute-start.46
  259.4 6.9 %collective-permute-done.46.refs_18_ = bf16[128,1024]{1,0:T(8,128)(2,1)S(1)} collective-permute-done((bf16[128,1024]{1,0:T(8,128)(2,1)S(1)}, bf16[128,1024]{1,0:T(8,128)(2,1)S(1)}, u32[]{:S(2)}, u32[]{:S(2)}) %collective-permute-start.46) | collective-permute-done | bytes 262176 | tf_op jit(solution)/shard_map/ppermute | solution.py:26
  268.0 1.5 collective-permute-start.56
  269.6 8.9 %collective-permute-done.56 = bf16[1376,128]{1,0:T(8,128)(2,1)S(1)} collective-permute-done((bf16[1376,128]{1,0:T(8,128)(2,1)S(1)}, bf16[1376,128]{1,0:T(8,128)(2,1)S(1)}, u32[]{:S(2)}, u32[]{:S(2)}) %collective-permute-start.56) | collective-permute-done | bytes 352288 | tf_op jit(solution)/shard_map/ppermute | solution.py:30
  278.6 1.5 collective-permute-done.47
  280.1 1.5 collective-permute-start.52
  281.7 8.7 %collective-permute-done.52 = bf16[1376,128]{1,0:T(8,128)(2,1)S(1)} collective-permute-done((bf16[1376,128]{1,0:T(8,128)(2,1)S(1)}, bf16[1376,128]{1,0:T(8,128)(2,1)S(1)}, u32[]{:S(2)}, u32[]{:S(2)}) %collective-permute-start.52) | collective-permute-done | bytes 352288 | tf_op jit(solution)/shard_map/ppermute | solution.py:30
  290.4 1.5 collective-permute-start.48
  292.0 7.8 %collective-permute-done.48 = bf16[1376,128]{1,0:T(8,128)(2,1)S(1)} collective-permute-done((bf16[1376,128]{1,0:T(8,128)(2,1)S(1)}, bf16[1376,128]{1,0:T(8,128)(2,1)S(1)}, u32[]{:S(2)}, u32[]{:S(2)}) %collective-permute-start.48) | collective-permute-done | bytes 352288 | tf_op jit(solution)/shard_map/ppermute | solution.py:30
  302.3 12.0 %down_grads.1 = (f32[688,1024]{1,0:T(8,128)}, f32[688,1024]{1,0:T(8,128)}, f32[8,128]{1,0:T(8,128)}) custom-call(s32[1]{0:T(128)} %bitcast.refs_0_, bf16[1376,1024]{1,0:T(8,128)(2,1)} %copy-done.38, bf16[688,1024]{1,0:T(8,128)(2,1)} %get-tuple-element.37.refs_2_, bf16[128,1024]{1,0:T(8,128)(2,1)} %copy-done.9, bf16[128,1024]{1,0:T(8,128)(2,1)} %copy-done.25, ...), custom_call_target="tpu_custom_call" | custom-call | flops 4328521728 | bytes 8454144 | tf_op jit(solution)/shard_map/down_grads/pallas_call | solution.py:144
  314.3 3.2 cotangents.4.refs_0_
  317.4 3.2 cotangents.5.refs_0_
  320.6 3.2 cotangents.6.refs_0_
  324.6 3.2 cotangents.7.refs_4_
  327.8 14.3 %wide_grads.1 = (f32[688,1024]{1,0:T(8,128)}, f32[688,1024]{1,0:T(8,128)}, f32[688,1024]{1,0:T(8,128)}, f32[688,1024]{1,0:T(8,128)}, f32[8,128]{1,0:T(8,128)}) custom-call(s32[1]{0:T(128)} %bitcast.refs_0_, bf16[688,1024]{1,0:T(8,128)(2,1)} %get-tuple-element.35.refs_1_, bf16[688,1024]{1,0:T(8,128)(2,1)} %get-tuple-element.36.refs_2_, ...), custom_call_target="tpu_custom_call" | custom-call | flops 5771362304 | bytes 14090240 | tf_op jit(solution)/shard_map/wide_grads/pallas_call | solution.py:196
  342.2 1.3 collective-permute-done.63
  344.2 1.5 collective-permute-start.64
  345.7 2.1 collective-permute-done.64
  348.8 2.6 collective-permute-done.65
  351.4 3.6 collective-permute-done.66
  355.0 4.5 %collective-permute-done.67 = f32[8,128]{1,0:T(8,128)S(1)} collective-permute-done((f32[8,128]{1,0:T(8,128)S(1)}, f32[8,128]{1,0:T(8,128)S(1)}, u32[]{:S(2)}, u32[]{:S(2)}) %collective-permute-start.67) | collective-permute-done | bytes 4128 | tf_op jit(solution)/shard_map/ppermute | solution.py:38
  360.1 21.7 %update.1 = (f32[688,1024]{1,0:T(8,128)}, f32[688,1024]{1,0:T(8,128)}, f32[688,1024]{1,0:T(8,128)}, f32[688,1024]{1,0:T(8,128)}, f32[688,1024]{1,0:T(8,128)}, /*...) custom-call(f32[2]{0:T(128)} %rsqrt_bitcast_fusion.scale_ref, ...), custom_call_target="tpu_custom_call" | custom-call | tf_op jit(solution)/shard_map/update/pallas_call | solution.py:272
  (322 shorter events, 59.3 us)
Async XLA Ops:
  0.7 10.4 %collective-permute-start.3 = (bf16[128,1024]{1,0:T(8,128)(2,1)}, bf16[128,1024]{1,0:T(8,128)(2,1)S(1)}, u32[]{:S(2)}, u32[]{:S(2)}) collective-permute-start(bf16[128,1024]{1,0:T(8,128)(2,1)} %refs_5_.1), channel_id=1, source_target_pairs={{0,1},{1,0},{2,3},{3,2},{4,5},{5,4},{6,7},{7,6},{8,9},{9,8},{10,11... | collective-permute-start | bytes 786440 | tf_op jit(solution)/shard_map/ppermute | solution.py:26
  3.7 12.9 %collective-permute-start = (bf16[128,1024]{1,0:T(8,128)(2,1)}, bf16[128,1024]{1,0:T(8,128)(2,1)S(1)}, u32[]{:S(2)}, u32[]{:S(2)}) collective-permute-start(bf16[128,1024]{1,0:T(8,128)(2,1)} %refs_5_.1), channel_id=1, source_target_pairs={{0,2},{1,3},{2,4},{3,5},{4,6},{5,7},{6,0},{7,1},{8,10},{9,11},{10,... | collective-permute-start | bytes 786440 | tf_op jit(solution)/shard_map/ppermute | solution.py:30
  16.6 7.5 %collective-permute-start.1 = (bf16[128,1024]{1,0:T(8,128)(2,1)S(1)}, bf16[128,1024]{1,0:T(8,128)(2,1)S(1)}, u32[]{:S(2)}, u32[]{:S(2)}) collective-permute-start(bf16[128,1024]{1,0:T(8,128)(2,1)S(1)} %collective-permute-done.refs_7_), channel_id=1, source_target_pairs={{0,1},{1,0},{2,3},{3,2},{4,5},{5,4},{6,7},{7,6},{8,9},{9,8},{10,11... | collective-permute-start | bytes 786440 | tf_op jit(solution)/shard_map/ppermute | solution.py:26
  17.7 34.0 %collective-permute-start.4 = (bf16[2752,128]{1,0:T(8,128)(2,1)S(1)}, bf16[2752,128]{1,0:T(8,128)(2,1)S(1)}, u32[]{:S(2)}, u32[]{:S(2)}) collective-permute-start(bf16[2752,128]{1,0:T(8,128)(2,1)S(1)} %pad_maximum_fusion.3), channel_id=1, source_target_pairs={{0,8},{8,0},{16,24},{24,16},{1,9},{9,1},{17,25},{25,17},{2,10},{10... | collective-permute-start | bytes 2113544 | tf_op jit(solution)/shard_map/ppermute | solution.py:26
  17.7 10.6 %collective-permute-start.8 = (bf16[128,1024]{1,0:T(8,128)(2,1)S(1)}, bf16[128,1024]{1,0:T(8,128)(2,1)S(1)}, u32[]{:S(2)}, u32[]{:S(2)}) collective-permute-start(bf16[128,1024]{1,0:T(8,128)(2,1)S(1)} %collective-permute-done.refs_7_), channel_id=1, source_target_pairs={{0,2},{1,3},{2,4},{3,5},{4,6},{5,7},{6,0},{7,1},{8,10},{9,11},{10,... | collective-permute-start | bytes 786440 | tf_op jit(solution)/shard_map/ppermute | solution.py:30
  28.3 7.9 %collective-permute-start.12 = (bf16[128,1024]{1,0:T(8,128)(2,1)S(1)}, bf16[128,1024]{1,0:T(8,128)(2,1)S(1)}, u32[]{:S(2)}, u32[]{:S(2)}) collective-permute-start(bf16[128,1024]{1,0:T(8,128)(2,1)S(1)} %collective-permute-done.8.refs_9_), channel_id=1, source_target_pairs={{0,1},{1,0},{2,3},{3,2},{4,5},{5,4},{6,7},{7,6},{8,9},{9,8},{10,11... | collective-permute-start | bytes 786440 | tf_op jit(solution)/shard_map/ppermute | solution.py:26
  29.4 22.2 %collective-permute-start.2 = (bf16[2752,128]{1,0:T(8,128)(2,1)S(1)}, bf16[2752,128]{1,0:T(8,128)(2,1)S(1)}, u32[]{:S(2)}, u32[]{:S(2)}) collective-permute-start(bf16[2752,128]{1,0:T(8,128)(2,1)S(1)} %pad_maximum_fusion.2), channel_id=1, source_target_pairs={{0,8},{8,0},{16,24},{24,16},{1,9},{9,1},{17,25},{25,17},{2,10},{10... | collective-permute-start | bytes 2113544 | tf_op jit(solution)/shard_map/ppermute | solution.py:26
  29.5 10.9 %collective-permute-start.9 = (bf16[128,1024]{1,0:T(8,128)(2,1)S(1)}, bf16[128,1024]{1,0:T(8,128)(2,1)S(1)}, u32[]{:S(2)}, u32[]{:S(2)}) collective-permute-start(bf16[128,1024]{1,0:T(8,128)(2,1)S(1)} %collective-permute-done.8.refs_9_), channel_id=1, source_target_pairs={{0,2},{1,3},{2,4},{3,5},{4,6},{5,7},{6,0},{7,1},{8,10},{9,11},{10,... | collective-permute-start | bytes 786440 | tf_op jit(solution)/shard_map/ppermute | solution.py:30
  40.4 7.8 %collective-permute-start.10 = (bf16[128,1024]{1,0:T(8,128)(2,1)S(1)}, bf16[128,1024]{1,0:T(8,128)(2,1)S(1)}, u32[]{:S(2)}, u32[]{:S(2)}) collective-permute-start(bf16[128,1024]{1,0:T(8,128)(2,1)S(1)} %collective-permute-done.9.refs_11_), channel_id=1, source_target_pairs={{0,1},{1,0},{2,3},{3,2},{4,5},{5,4},{6,7},{7,6},{8,9},{9,8},{10,11... | collective-permute-start | bytes 786440 | tf_op jit(solution)/shard_map/ppermute | solution.py:26
  41.5 12.1 %collective-permute-start.13 = (bf16[2752,128]{1,0:T(8,128)(2,1)S(1)}, bf16[2752,128]{1,0:T(8,128)(2,1)S(1)}, u32[]{:S(2)}, u32[]{:S(2)}) collective-permute-start(bf16[2752,128]{1,0:T(8,128)(2,1)S(1)} %pad_maximum_fusion.5), channel_id=1, source_target_pairs={{0,8},{8,0},{16,24},{24,16},{1,9},{9,1},{17,25},{25,17},{2,10},{10... | collective-permute-start | bytes 2113544 | tf_op jit(solution)/shard_map/ppermute | solution.py:26
  51.6 2.2 collective-permute-start.11
  52.0 18.7 %collective-permute-start.5 = (bf16[2752,128]{1,0:T(8,128)(2,1)S(1)}, bf16[2752,128]{1,0:T(8,128)(2,1)S(1)}, u32[]{:S(2)}, u32[]{:S(2)}) collective-permute-start(bf16[2752,128]{1,0:T(8,128)(2,1)S(1)} %select_convert_fusion.1), channel_id=1, source_target_pairs={{0,16},{8,24},{16,0},{24,8},{1,17},{9,25},{17,1},{25,9},{2,18},{10... | collective-permute-start | bytes 2113544 | tf_op jit(solution)/shard_map/ppermute | solution.py:30
  54.1 42.0 %collective-permute-start.14 = (bf16[2752,128]{1,0:T(8,128)(2,1)S(1)}, bf16[2752,128]{1,0:T(8,128)(2,1)S(1)}, u32[]{:S(2)}, u32[]{:S(2)}) collective-permute-start(bf16[2752,128]{1,0:T(8,128)(2,1)S(1)} %select_convert_fusion), channel_id=1, source_target_pairs={{0,16},{8,24},{16,0},{24,8},{1,17},{9,25},{17,1},{25,9},{2,18},{10... | collective-permute-start | bytes 2113544 | tf_op jit(solution)/shard_map/ppermute | solution.py:30
  71.5 21.8 %collective-permute-start.6 = (bf16[1376,128]{1,0:T(8,128)(2,1)S(1)}, bf16[1376,128]{1,0:T(8,128)(2,1)S(1)}, u32[]{:S(2)}, u32[]{:S(2)}) collective-permute-start(bf16[1376,128]{1,0:T(8,128)(2,1)S(1)} %pad_maximum_fusion.16), channel_id=1, source_target_pairs={{0,16},{8,24},{16,0},{24,8},{1,17},{9,25},{17,1},{25,9},{2,18},{10... | collective-permute-start | bytes 1056776 | tf_op jit(solution)/shard_map/ppermute | solution.py:30
  73.1 110.7 %collective-permute-start.24 = (bf16[2752,128]{1,0:T(8,128)(2,1)S(1)}, bf16[2752,128]{1,0:T(8,128)(2,1)S(1)}, u32[]{:S(2)}, u32[]{:S(2)}) collective-permute-start(bf16[2752,128]{1,0:T(8,128)(2,1)S(1)} %pad_maximum_fusion.6), channel_id=1, source_target_pairs={{0,16},{8,24},{16,0},{24,8},{1,17},{9,25},{17,1},{25,9},{2,18},{10... | collective-permute-start | bytes 2113544 | tf_op jit(solution)/shard_map/ppermute | solution.py:30
  93.6 5.6 %collective-permute-start.7 = (bf16[1376,256]{1,0:T(8,128)(2,1)S(1)}, bf16[1376,256]{1,0:T(8,128)(2,1)S(1)}, u32[]{:S(2)}, u32[]{:S(2)}) collective-permute-start(bf16[1376,256]{1,0:T(8,128)(2,1)S(1)} %pad_maximum_fusion), channel_id=1, source_target_pairs={{0,8},{8,0},{16,24},{24,16},{1,9},{9,1},{17,25},{25,17},{2,10},{10... | collective-permute-start | bytes 2113544 | tf_op jit(solution)/shard_map/ppermute | solution.py:26
  96.9 19.0 %collective-permute-start.15 = (bf16[1376,128]{1,0:T(8,128)(2,1)S(1)}, bf16[1376,128]{1,0:T(8,128)(2,1)S(1)}, u32[]{:S(2)}, u32[]{:S(2)}) collective-permute-start(bf16[1376,128]{1,0:T(8,128)(2,1)S(1)} %pad_maximum_fusion.17), channel_id=1, source_target_pairs={{0,16},{8,24},{16,0},{24,8},{1,17},{9,25},{17,1},{25,9},{2,18},{10... | collective-permute-start | bytes 1056776 | tf_op jit(solution)/shard_map/ppermute | solution.py:30
  98.5 85.3 %collective-permute-start.25 = (bf16[2752,128]{1,0:T(8,128)(2,1)S(1)}, bf16[2752,128]{1,0:T(8,128)(2,1)S(1)}, u32[]{:S(2)}, u32[]{:S(2)}) collective-permute-start(bf16[2752,128]{1,0:T(8,128)(2,1)S(1)} %pad_maximum_fusion.7), channel_id=1, source_target_pairs={{0,16},{8,24},{16,0},{24,8},{1,17},{9,25},{17,1},{25,9},{2,18},{10... | collective-permute-start | bytes 2113544 | tf_op jit(solution)/shard_map/ppermute | solution.py:30
  117.5 20.9 %collective-permute-start.16 = (bf16[1376,256]{1,0:T(8,128)(2,1)S(1)}, bf16[1376,256]{1,0:T(8,128)(2,1)S(1)}, u32[]{:S(2)}, u32[]{:S(2)}) collective-permute-start(bf16[1376,256]{1,0:T(8,128)(2,1)S(1)} %pad_maximum_fusion.1), channel_id=1, source_target_pairs={{0,8},{8,0},{16,24},{24,16},{1,9},{9,1},{17,25},{25,17},{2,10},{10... | collective-permute-start | bytes 2113544 | tf_op jit(solution)/shard_map/ppermute | solution.py:26
  118.3 9.2 %collective-permute-start.17 = (bf16[128,1024]{1,0:T(8,128)(2,1)S(1)}, bf16[128,1024]{1,0:T(8,128)(2,1)S(1)}, u32[]{:S(2)}, u32[]{:S(2)}) collective-permute-start(bf16[128,1024]{1,0:T(8,128)(2,1)S(1)} %get-tuple-element.69), channel_id=1, source_target_pairs={{0,1},{1,0},{2,3},{3,2},{4,5},{5,4},{6,7},{7,6},{8,9},{9,8},{10,11... | collective-permute-start | bytes 786440 | tf_op jit(solution)/shard_map/ppermute | solution.py:26
  119.4 55.1 %collective-permute-start.23 = (bf16[128,1024]{1,0:T(8,128)(2,1)S(1)}, bf16[128,1024]{1,0:T(8,128)(2,1)S(1)}, u32[]{:S(2)}, u32[]{:S(2)}) collective-permute-start(bf16[128,1024]{1,0:T(8,128)(2,1)S(1)} %get-tuple-element.70), channel_id=1, source_target_pairs={{0,1},{1,0},{2,3},{3,2},{4,5},{5,4},{6,7},{7,6},{8,9},{9,8},{10,11... | collective-permute-start | bytes 786440 | tf_op jit(solution)/shard_map/ppermute | solution.py:26
  127.5 10.8 %collective-permute-start.33 = (bf16[128,1024]{1,0:T(8,128)(2,1)S(1)}, bf16[128,1024]{1,0:T(8,128)(2,1)S(1)}, u32[]{:S(2)}, u32[]{:S(2)}) collective-permute-start(bf16[128,1024]{1,0:T(8,128)(2,1)S(1)} %get-tuple-element.65), channel_id=1, source_target_pairs={{0,1},{1,0},{2,3},{3,2},{4,5},{5,4},{6,7},{7,6},{8,9},{9,8},{10,11... | collective-permute-start | bytes 786440 | tf_op jit(solution)/shard_map/ppermute | solution.py:26
  138.3 9.6 %collective-permute-start.18 = (bf16[128,1024]{1,0:T(8,128)(2,1)S(1)}, bf16[128,1024]{1,0:T(8,128)(2,1)S(1)}, u32[]{:S(2)}, u32[]{:S(2)}) collective-permute-start(bf16[128,1024]{1,0:T(8,128)(2,1)S(1)} %add_convert_fusion.10), channel_id=1, source_target_pairs={{0,2},{1,3},{2,4},{3,5},{4,6},{5,7},{6,0},{7,1},{8,10},{9,11},{10,... | collective-permute-start | bytes 786440 | tf_op jit(solution)/shard_map/ppermute | solution.py:30
  139.4 8.6 %collective-permute-start.19 = (bf16[128,1024]{1,0:T(8,128)(2,1)S(1)}, bf16[128,1024]{1,0:T(8,128)(2,1)S(1)}, u32[]{:S(2)}, u32[]{:S(2)}) collective-permute-start(bf16[128,1024]{1,0:T(8,128)(2,1)S(1)} %get-tuple-element.71), channel_id=1, source_target_pairs={{0,1},{1,0},{2,3},{3,2},{4,5},{5,4},{6,7},{7,6},{8,9},{9,8},{10,11... | collective-permute-start | bytes 786440 | tf_op jit(solution)/shard_map/ppermute | solution.py:26
  147.9 8.8 %collective-permute-start.34 = (bf16[128,1024]{1,0:T(8,128)(2,1)S(1)}, bf16[128,1024]{1,0:T(8,128)(2,1)S(1)}, u32[]{:S(2)}, u32[]{:S(2)}) collective-permute-start(bf16[128,1024]{1,0:T(8,128)(2,1)S(1)} %add_convert_fusion.7), channel_id=1, source_target_pairs={{0,2},{1,3},{2,4},{3,5},{4,6},{5,7},{6,0},{7,1},{8,10},{9,11},{10,... | collective-permute-start | bytes 786440 | tf_op jit(solution)/shard_map/ppermute | solution.py:30
  148.0 9.8 %collective-permute-start.35 = (bf16[128,1024]{1,0:T(8,128)(2,1)S(1)}, bf16[128,1024]{1,0:T(8,128)(2,1)S(1)}, u32[]{:S(2)}, u32[]{:S(2)}) collective-permute-start(bf16[128,1024]{1,0:T(8,128)(2,1)S(1)} %get-tuple-element.67), channel_id=1, source_target_pairs={{0,1},{1,0},{2,3},{3,2},{4,5},{5,4},{6,7},{7,6},{8,9},{9,8},{10,11... | collective-permute-start | bytes 786440 | tf_op jit(solution)/shard_map/ppermute | solution.py:26
  156.7 7.0 %collective-permute-start.21 = (bf16[128,1024]{1,0:T(8,128)(2,1)S(1)}, bf16[128,1024]{1,0:T(8,128)(2,1)S(1)}, u32[]{:S(2)}, u32[]{:S(2)}) collective-permute-start(bf16[128,1024]{1,0:T(8,128)(2,1)S(1)} %get-tuple-element.72), channel_id=1, source_target_pairs={{0,1},{1,0},{2,3},{3,2},{4,5},{5,4},{6,7},{7,6},{8,9},{9,8},{10,11... | collective-permute-start | bytes 786440 | tf_op jit(solution)/shard_map/ppermute | solution.py:26
  157.7 8.2 %collective-permute-start.20 = (bf16[128,1024]{1,0:T(8,128)(2,1)S(1)}, bf16[128,1024]{1,0:T(8,128)(2,1)S(1)}, u32[]{:S(2)}, u32[]{:S(2)}) collective-permute-start(bf16[128,1024]{1,0:T(8,128)(2,1)S(1)} %add_convert_fusion.9), channel_id=1, source_target_pairs={{0,2},{1,3},{2,4},{3,5},{4,6},{5,7},{6,0},{7,1},{8,10},{9,11},{10,... | collective-permute-start | bytes 786440 | tf_op jit(solution)/shard_map/ppermute | solution.py:30
  163.7 7.9 %collective-permute-start.37 = (bf16[128,1024]{1,0:T(8,128)(2,1)S(1)}, bf16[128,1024]{1,0:T(8,128)(2,1)S(1)}, u32[]{:S(2)}, u32[]{:S(2)}) collective-permute-start(bf16[128,1024]{1,0:T(8,128)(2,1)S(1)} %get-tuple-element.68), channel_id=1, source_target_pairs={{0,1},{1,0},{2,3},{3,2},{4,5},{5,4},{6,7},{7,6},{8,9},{9,8},{10,11... | collective-permute-start | bytes 786440 | tf_op jit(solution)/shard_map/ppermute | solution.py:26
  165.9 8.4 %collective-permute-start.36 = (bf16[128,1024]{1,0:T(8,128)(2,1)S(1)}, bf16[128,1024]{1,0:T(8,128)(2,1)S(1)}, u32[]{:S(2)}, u32[]{:S(2)}) collective-permute-start(bf16[128,1024]{1,0:T(8,128)(2,1)S(1)} %add_convert_fusion.6), channel_id=1, source_target_pairs={{0,2},{1,3},{2,4},{3,5},{4,6},{5,7},{6,0},{7,1},{8,10},{9,11},{10,... | collective-permute-start | bytes 786440 | tf_op jit(solution)/shard_map/ppermute | solution.py:30
  171.6 13.4 %collective-permute-start.39 = (bf16[128,1024]{1,0:T(8,128)(2,1)S(1)}, bf16[128,1024]{1,0:T(8,128)(2,1)S(1)}, u32[]{:S(2)}, u32[]{:S(2)}) collective-permute-start(bf16[128,1024]{1,0:T(8,128)(2,1)S(1)} %get-tuple-element.66), channel_id=1, source_target_pairs={{0,1},{1,0},{2,3},{3,2},{4,5},{5,4},{6,7},{7,6},{8,9},{9,8},{10,11... | collective-permute-start | bytes 786440 | tf_op jit(solution)/shard_map/ppermute | solution.py:26
  174.3 9.3 %collective-permute-start.22 = (bf16[128,1024]{1,0:T(8,128)(2,1)S(1)}, bf16[128,1024]{1,0:T(8,128)(2,1)S(1)}, u32[]{:S(2)}, u32[]{:S(2)}) collective-permute-start(bf16[128,1024]{1,0:T(8,128)(2,1)S(1)} %add_convert_fusion.8), channel_id=1, source_target_pairs={{0,2},{1,3},{2,4},{3,5},{4,6},{5,7},{6,0},{7,1},{8,10},{9,11},{10,... | collective-permute-start | bytes 786440 | tf_op jit(solution)/shard_map/ppermute | solution.py:30
  174.5 14.7 %collective-permute-start.38 = (bf16[128,1024]{1,0:T(8,128)(2,1)S(1)}, bf16[128,1024]{1,0:T(8,128)(2,1)S(1)}, u32[]{:S(2)}, u32[]{:S(2)}) collective-permute-start(bf16[128,1024]{1,0:T(8,128)(2,1)S(1)} %add_convert_fusion.5), channel_id=1, source_target_pairs={{0,2},{1,3},{2,4},{3,5},{4,6},{5,7},{6,0},{7,1},{8,10},{9,11},{10,... | collective-permute-start | bytes 786440 | tf_op jit(solution)/shard_map/ppermute | solution.py:30
  183.9 12.8 %collective-permute-start.27 = (bf16[128,1024]{1,0:T(8,128)(2,1)S(1)}, bf16[128,1024]{1,0:T(8,128)(2,1)S(1)}, u32[]{:S(2)}, u32[]{:S(2)}) collective-permute-start(bf16[128,1024]{1,0:T(8,128)(2,1)S(1)} %subtract_convert_fusion.refs_3_), channel_id=1, source_target_pairs={{0,2},{1,3},{2,4},{3,5},{4,6},{5,7},{6,0},{7,1},{8,10},{9,11},{10,... | collective-permute-start | bytes 786440 | tf_op jit(solution)/shard_map/ppermute | solution.py:30
  183.9 7.7 %collective-permute-start.26 = (bf16[128,1024]{1,0:T(8,128)(2,1)S(1)}, bf16[128,1024]{1,0:T(8,128)(2,1)S(1)}, u32[]{:S(2)}, u32[]{:S(2)}) collective-permute-start(bf16[128,1024]{1,0:T(8,128)(2,1)S(1)} %subtract_convert_fusion.refs_3_), channel_id=1, source_target_pairs={{0,1},{1,0},{2,3},{3,2},{4,5},{5,4},{6,7},{7,6},{8,9},{9,8},{10,11... | collective-permute-start | bytes 786440 | tf_op jit(solution)/shard_map/ppermute | solution.py:26
  189.4 9.0 %collective-permute-start.41 = (bf16[128,1024]{1,0:T(8,128)(2,1)S(1)}, bf16[128,1024]{1,0:T(8,128)(2,1)S(1)}, u32[]{:S(2)}, u32[]{:S(2)}) collective-permute-start(bf16[128,1024]{1,0:T(8,128)(2,1)S(1)} %add_convert_fusion.4.refs_11_), channel_id=1, source_target_pairs={{0,2},{1,3},{2,4},{3,5},{4,6},{5,7},{6,0},{7,1},{8,10},{9,11},{10,... | collective-permute-start | bytes 786440 | tf_op jit(solution)/shard_map/ppermute | solution.py:30
  189.5 6.4 %collective-permute-start.40 = (bf16[128,1024]{1,0:T(8,128)(2,1)S(1)}, bf16[128,1024]{1,0:T(8,128)(2,1)S(1)}, u32[]{:S(2)}, u32[]{:S(2)}) collective-permute-start(bf16[128,1024]{1,0:T(8,128)(2,1)S(1)} %add_convert_fusion.4.refs_11_), channel_id=1, source_target_pairs={{0,1},{1,0},{2,3},{3,2},{4,5},{5,4},{6,7},{7,6},{8,9},{9,8},{10,11... | collective-permute-start | bytes 786440 | tf_op jit(solution)/shard_map/ppermute | solution.py:26
  191.5 129.1 %collective-permute-start.54 = (bf16[2752,128]{1,0:T(8,128)(2,1)}, bf16[2752,128]{1,0:T(8,128)(2,1)}, u32[]{:S(2)}, u32[]{:S(2)}) collective-permute-start(bf16[2752,128]{1,0:T(8,128)(2,1)} %get-tuple-element.75.by_keep_ref), channel_id=1, source_target_pairs={{0,8},{8,0},{16,24},{24,16},{1,9},{9,1},{17,25},{25,17},{2,10},{10... | collective-permute-start | bytes 2113544 | tf_op jit(solution)/shard_map/ppermute | solution.py:26
  192.5 131.3 %collective-permute-start.50 = (bf16[2752,128]{1,0:T(8,128)(2,1)S(1)}, bf16[2752,128]{1,0:T(8,128)(2,1)}, u32[]{:S(2)}, u32[]{:S(2)}) collective-permute-start(bf16[2752,128]{1,0:T(8,128)(2,1)S(1)} %get-tuple-element.76.by_keep_ref), channel_id=1, source_target_pairs={{0,8},{8,0},{16,24},{24,16},{1,9},{9,1},{17,25},{25,17},{2,10},{10... | collective-permute-start | bytes 2113544 | tf_op jit(solution)/shard_map/ppermute | solution.py:26
  195.9 104.1 %collective-permute-start.62 = (bf16[2752,128]{1,0:T(8,128)(2,1)S(1)}, bf16[2752,128]{1,0:T(8,128)(2,1)S(1)}, u32[]{:S(2)}, u32[]{:S(2)}) collective-permute-start(bf16[2752,128]{1,0:T(8,128)(2,1)S(1)} %get-tuple-element.73.by_keep_ref), channel_id=1, source_target_pairs={{0,8},{8,0},{16,24},{24,16},{1,9},{9,1},{17,25},{25,17},{2,10},{10... | collective-permute-start | bytes 2113544 | tf_op jit(solution)/shard_map/ppermute | solution.py:26
  196.6 8.7 %collective-permute-start.28 = (bf16[128,1024]{1,0:T(8,128)(2,1)S(1)}, bf16[128,1024]{1,0:T(8,128)(2,1)S(1)}, u32[]{:S(2)}, u32[]{:S(2)}) collective-permute-start(bf16[128,1024]{1,0:T(8,128)(2,1)S(1)} %collective-permute-done.27.refs_5_), channel_id=1, source_target_pairs={{0,1},{1,0},{2,3},{3,2},{4,5},{5,4},{6,7},{7,6},{8,9},{9,8},{10,11... | collective-permute-start | bytes 786440 | tf_op jit(solution)/shard_map/ppermute | solution.py:26
  198.5 23.7 %collective-permute-start.59 = (bf16[1376,128]{1,0:T(8,128)(2,1)S(1)}, bf16[1376,128]{1,0:T(8,128)(2,1)S(1)}, u32[]{:S(2)}, u32[]{:S(2)}) collective-permute-start(bf16[1376,128]{1,0:T(8,128)(2,1)S(1)} %pad_maximum_fusion.21), channel_id=1, source_target_pairs={{0,8},{8,0},{16,24},{24,16},{1,9},{9,1},{17,25},{25,17},{2,10},{10... | collective-permute-start | bytes 1056776 | tf_op jit(solution)/shard_map/ppermute | solution.py:26
  205.4 7.8 %collective-permute-start.42 = (bf16[128,1024]{1,0:T(8,128)(2,1)S(1)}, bf16[128,1024]{1,0:T(8,128)(2,1)S(1)}, u32[]{:S(2)}, u32[]{:S(2)}) collective-permute-start(bf16[128,1024]{1,0:T(8,128)(2,1)S(1)} %collective-permute-done.41.refs_13_), channel_id=1, source_target_pairs={{0,1},{1,0},{2,3},{3,2},{4,5},{5,4},{6,7},{7,6},{8,9},{9,8},{10,11... | collective-permute-start | bytes 786440 | tf_op jit(solution)/shard_map/ppermute | solution.py:26
  213.2 9.0 %collective-permute-start.29 = (bf16[128,1024]{1,0:T(8,128)(2,1)S(1)}, bf16[128,1024]{1,0:T(8,128)(2,1)S(1)}, u32[]{:S(2)}, u32[]{:S(2)}) collective-permute-start(bf16[128,1024]{1,0:T(8,128)(2,1)S(1)} %collective-permute-done.27.refs_5_), channel_id=1, source_target_pairs={{0,2},{1,3},{2,4},{3,5},{4,6},{5,7},{6,0},{7,1},{8,10},{9,11},{10,... | collective-permute-start | bytes 786440 | tf_op jit(solution)/shard_map/ppermute | solution.py:30
  222.2 8.2 %collective-permute-start.43 = (bf16[128,1024]{1,0:T(8,128)(2,1)S(1)}, bf16[128,1024]{1,0:T(8,128)(2,1)S(1)}, u32[]{:S(2)}, u32[]{:S(2)}) collective-permute-start(bf16[128,1024]{1,0:T(8,128)(2,1)S(1)} %collective-permute-done.41.refs_13_), channel_id=1, source_target_pairs={{0,2},{1,3},{2,4},{3,5},{4,6},{5,7},{6,0},{7,1},{8,10},{9,11},{10,... | collective-permute-start | bytes 786440 | tf_op jit(solution)/shard_map/ppermute | solution.py:30
  222.2 8.2 %collective-permute-start.30 = (bf16[128,1024]{1,0:T(8,128)(2,1)S(1)}, bf16[128,1024]{1,0:T(8,128)(2,1)S(1)}, u32[]{:S(2)}, u32[]{:S(2)}) collective-permute-start(bf16[128,1024]{1,0:T(8,128)(2,1)S(1)} %collective-permute-done.29.refs_7_), channel_id=1, source_target_pairs={{0,1},{1,0},{2,3},{3,2},{4,5},{5,4},{6,7},{7,6},{8,9},{9,8},{10,11... | collective-permute-start | bytes 786440 | tf_op jit(solution)/shard_map/ppermute | solution.py:26
  230.4 10.2 %collective-permute-start.55 = (bf16[1376,128]{1,0:T(8,128)(2,1)S(1)}, bf16[1376,128]{1,0:T(8,128)(2,1)S(1)}, u32[]{:S(2)}, u32[]{:S(2)}) collective-permute-start(bf16[1376,128]{1,0:T(8,128)(2,1)S(1)} %pad_maximum_fusion.20), channel_id=1, source_target_pairs={{0,8},{8,0},{16,24},{24,16},{1,9},{9,1},{17,25},{25,17},{2,10},{10... | collective-permute-start | bytes 1056776 | tf_op jit(solution)/shard_map/ppermute | solution.py:26
  230.4 8.7 %collective-permute-start.44 = (bf16[128,1024]{1,0:T(8,128)(2,1)S(1)}, bf16[128,1024]{1,0:T(8,128)(2,1)S(1)}, u32[]{:S(2)}, u32[]{:S(2)}) collective-permute-start(bf16[128,1024]{1,0:T(8,128)(2,1)S(1)} %collective-permute-done.43.refs_15_), channel_id=1, source_target_pairs={{0,1},{1,0},{2,3},{3,2},{4,5},{5,4},{6,7},{7,6},{8,9},{9,8},{10,11... | collective-permute-start | bytes 786440 | tf_op jit(solution)/shard_map/ppermute | solution.py:26
  239.1 9.6 %collective-permute-start.31 = (bf16[128,1024]{1,0:T(8,128)(2,1)S(1)}, bf16[128,1024]{1,0:T(8,128)(2,1)S(1)}, u32[]{:S(2)}, u32[]{:S(2)}) collective-permute-start(bf16[128,1024]{1,0:T(8,128)(2,1)S(1)} %collective-permute-done.29.refs_7_), channel_id=1, source_target_pairs={{0,2},{1,3},{2,4},{3,5},{4,6},{5,7},{6,0},{7,1},{8,10},{9,11},{10,... | collective-permute-start | bytes 786440 | tf_op jit(solution)/shard_map/ppermute | solution.py:30
  240.6 9.8 %collective-permute-start.60 = (bf16[1376,128]{1,0:T(8,128)(2,1)S(1)}, bf16[1376,128]{1,0:T(8,128)(2,1)S(1)}, u32[]{:S(2)}, u32[]{:S(2)}) collective-permute-start(bf16[1376,128]{1,0:T(8,128)(2,1)S(1)} %fusion.16), channel_id=1, source_target_pairs={{0,16},{8,24},{16,0},{24,8},{1,17},{9,25},{17,1},{25,9},{2,18},{10... | collective-permute-start | bytes 1056776 | tf_op jit(solution)/shard_map/ppermute | solution.py:30
  248.7 8.9 %collective-permute-start.45 = (bf16[128,1024]{1,0:T(8,128)(2,1)S(1)}, bf16[128,1024]{1,0:T(8,128)(2,1)S(1)}, u32[]{:S(2)}, u32[]{:S(2)}) collective-permute-start(bf16[128,1024]{1,0:T(8,128)(2,1)S(1)} %collective-permute-done.43.refs_15_), channel_id=1, source_target_pairs={{0,2},{1,3},{2,4},{3,5},{4,6},{5,7},{6,0},{7,1},{8,10},{9,11},{10,... | collective-permute-start | bytes 786440 | tf_op jit(solution)/shard_map/ppermute | solution.py:30
  250.4 7.3 %collective-permute-start.32 = (bf16[128,1024]{1,0:T(8,128)(2,1)S(1)}, bf16[128,1024]{1,0:T(8,128)(2,1)S(1)}, u32[]{:S(2)}, u32[]{:S(2)}) collective-permute-start(bf16[128,1024]{1,0:T(8,128)(2,1)S(1)} %collective-permute-done.31.refs_9_), channel_id=1, source_target_pairs={{0,1},{1,0},{2,3},{3,2},{4,5},{5,4},{6,7},{7,6},{8,9},{9,8},{10,11... | collective-permute-start | bytes 786440 | tf_op jit(solution)/shard_map/ppermute | solution.py:26
  257.6 43.0 %collective-permute-start.58 = (bf16[2752,128]{1,0:T(8,128)(2,1)S(1)}, bf16[2752,128]{1,0:T(8,128)(2,1)S(1)}, u32[]{:S(2)}, u32[]{:S(2)}) collective-permute-start(bf16[2752,128]{1,0:T(8,128)(2,1)S(1)} %get-tuple-element.74.by_keep_ref), channel_id=1, source_target_pairs={{0,8},{8,0},{16,24},{24,16},{1,9},{9,1},{17,25},{25,17},{2,10},{10... | collective-permute-start | bytes 2113544 | tf_op jit(solution)/shard_map/ppermute | solution.py:26
  257.6 8.7 %collective-permute-start.46 = (bf16[128,1024]{1,0:T(8,128)(2,1)S(1)}, bf16[128,1024]{1,0:T(8,128)(2,1)S(1)}, u32[]{:S(2)}, u32[]{:S(2)}) collective-permute-start(bf16[128,1024]{1,0:T(8,128)(2,1)S(1)} %collective-permute-done.45.refs_17_), channel_id=1, source_target_pairs={{0,1},{1,0},{2,3},{3,2},{4,5},{5,4},{6,7},{7,6},{8,9},{9,8},{10,11... | collective-permute-start | bytes 786440 | tf_op jit(solution)/shard_map/ppermute | solution.py:26
  268.0 10.5 %collective-permute-start.56 = (bf16[1376,128]{1,0:T(8,128)(2,1)S(1)}, bf16[1376,128]{1,0:T(8,128)(2,1)S(1)}, u32[]{:S(2)}, u32[]{:S(2)}) collective-permute-start(bf16[1376,128]{1,0:T(8,128)(2,1)S(1)} %fusion.17), channel_id=1, source_target_pairs={{0,16},{8,24},{16,0},{24,8},{1,17},{9,25},{17,1},{25,9},{2,18},{10... | collective-permute-start | bytes 1056776 | tf_op jit(solution)/shard_map/ppermute | solution.py:30
  280.1 10.3 %collective-permute-start.52 = (bf16[1376,128]{1,0:T(8,128)(2,1)S(1)}, bf16[1376,128]{1,0:T(8,128)(2,1)S(1)}, u32[]{:S(2)}, u32[]{:S(2)}) collective-permute-start(bf16[1376,128]{1,0:T(8,128)(2,1)S(1)} %fusion.18), channel_id=1, source_target_pairs={{0,16},{8,24},{16,0},{24,8},{1,17},{9,25},{17,1},{25,9},{2,18},{10... | collective-permute-start | bytes 1056776 | tf_op jit(solution)/shard_map/ppermute | solution.py:30
  290.4 9.4 %collective-permute-start.48 = (bf16[1376,128]{1,0:T(8,128)(2,1)S(1)}, bf16[1376,128]{1,0:T(8,128)(2,1)S(1)}, u32[]{:S(2)}, u32[]{:S(2)}) collective-permute-start(bf16[1376,128]{1,0:T(8,128)(2,1)S(1)} %fusion.19), channel_id=1, source_target_pairs={{0,16},{8,24},{16,0},{24,8},{1,17},{9,25},{17,1},{25,9},{2,18},{10... | collective-permute-start | bytes 1056776 | tf_op jit(solution)/shard_map/ppermute | solution.py:30
  300.0 17.4 %collective-permute-start.57 = (bf16[1376,128]{1,0:T(8,128)(2,1)S(1)}, bf16[1376,128]{1,0:T(8,128)(2,1)}, u32[]{:S(2)}, u32[]{:S(2)}) collective-permute-start(bf16[1376,128]{1,0:T(8,128)(2,1)S(1)} %add_convert_fusion.1.keep_ref), channel_id=1, source_target_pairs={{0,8},{8,0},{16,24},{24,16},{1,9},{9,1},{17,25},{25,17},{2,10},{10... | collective-permute-start | bytes 1056776 | tf_op jit(solution)/shard_map/ppermute | solution.py:26
  300.6 20.1 %collective-permute-start.53 = (bf16[1376,128]{1,0:T(8,128)(2,1)S(1)}, bf16[1376,128]{1,0:T(8,128)(2,1)}, u32[]{:S(2)}, u32[]{:S(2)}) collective-permute-start(bf16[1376,128]{1,0:T(8,128)(2,1)S(1)} %add_convert_fusion.2.keep_ref), channel_id=1, source_target_pairs={{0,8},{8,0},{16,24},{24,16},{1,9},{9,1},{17,25},{25,17},{2,10},{10... | collective-permute-start | bytes 1056776 | tf_op jit(solution)/shard_map/ppermute | solution.py:26
  301.5 22.3 %collective-permute-start.49 = (bf16[1376,128]{1,0:T(8,128)(2,1)S(1)}, bf16[1376,128]{1,0:T(8,128)(2,1)S(1)}, u32[]{:S(2)}, u32[]{:S(2)}) collective-permute-start(bf16[1376,128]{1,0:T(8,128)(2,1)S(1)} %add_convert_fusion.3.keep_ref), channel_id=1, source_target_pairs={{0,8},{8,0},{16,24},{24,16},{1,9},{9,1},{17,25},{25,17},{2,10},{10... | collective-permute-start | bytes 1056776 | tf_op jit(solution)/shard_map/ppermute | solution.py:26
  344.2 3.6 collective-permute-start.64
  347.8 3.6 collective-permute-start.65
  351.4 3.6 collective-permute-start.66
  355.0 4.5 %collective-permute-start.67 = (f32[8,128]{1,0:T(8,128)S(1)}, f32[8,128]{1,0:T(8,128)S(1)}, u32[]{:S(2)}, u32[]{:S(2)}) collective-permute-start(f32[8,128]{1,0:T(8,128)S(1)} %add.237), channel_id=1, source_target_pairs={{0,4},{1,5},{2,6},{3,7},{4,0},{5,1},{6,2},{7,3},{8,12},{9,13},{10,... | collective-permute-start | bytes 12296 | tf_op jit(solution)/shard_map/ppermute | solution.py:38
  (47 other events, 469.8 us)

commit v2 on v1

v2 whole, which is shorter than its diff:
```python
import jax
import jax.numpy as jnp
from jax import lax
from jax.experimental import pallas as pl
from jax.experimental.pallas import tpu as pltpu
from jax.sharding import PartitionSpec as P


STEP = 10
BF = jnp.bfloat16
F32 = jnp.float32


def dot(left, right, inner):
    return lax.dot_general(left, right, (((inner[0],), (inner[1],)), ((), ())), preferred_element_type=F32)


def pick(blocks, index):
    chosen = blocks[0]
    for at in range(1, len(blocks)):
        chosen = jnp.where(index == at, blocks[at], chosen)
    return chosen


def pair_swap(value, axis, size):
    return lax.ppermute(value, axis, [(i, i ^ 1) for i in range(size)])


def ring_up(value, axis, size):
    return lax.ppermute(value, axis, [(i, (i + 2) % size) for i in range(size)])


def ring_up_apart(value, n_row, n_col):
    perm = []
    for r in range(n_row):
        for c in range(n_col):
            perm.append((r * n_col + c, r * n_col + ((c + 2) % n_col ^ (r % 2))))
    return lax.ppermute(value, ("row", "col"), perm)


def total_over_all(value, sizes):
    for axis, size in sizes:
        step = 1
        while step < size:
            if size % (2 * step) == 0:
                value = value + lax.ppermute(value, axis, [(i, i ^ step) for i in range(size)])
                step *= 2
            else:
                raise ValueError("axis size")
    return value


def sign_kernel(gate_ref, up_ref, probe_gate_ref, probe_up_ref, probe_down_ref, wide_ref, down_ref):
    width = gate_ref.shape[0]
    wide_ref[:width] = gate_ref[...]
    wide_ref[width : 2 * width] = up_ref[...]
    for at, probe in ((2, probe_gate_ref), (3, probe_up_ref)):
        wide_ref[at * width : (at + 1) * width] = (2 * probe[...] - 1).astype(F32).astype(BF)
    down_ref[...] = (2 * probe_down_ref[...] - 1).astype(F32).astype(BF)


def side(feats, best=512):
    while feats % best:
        best //= 2
    return best


def cols_tile(rows, tile):
    return pl.BlockSpec((rows, tile), lambda i: (0, i))


def fixed(shape):
    return pl.BlockSpec(shape, lambda i: (0, 0))


def signs(*arrays):
    width, feats = arrays[0].shape
    tile = side(feats, 256)
    return pl.pallas_call(
        sign_kernel,
        grid=(feats // tile,),
        in_specs=[cols_tile(width, tile)] * 5,
        out_specs=[cols_tile(4 * width, tile), cols_tile(width, tile)],
        out_shape=[jax.ShapeDtypeStruct((n * width, feats), BF) for n in (4, 1)],
        name="signs",
    )(*arrays)


def same_block():
    down = lax.broadcasted_iota(jnp.int32, (256, 256), 0) >> 2
    across = lax.broadcasted_iota(jnp.int32, (256, 256), 1) >> 2
    return jnp.where(down == across, 1.0, 0.0).astype(BF)


def finish_weight(grad, hess, sign, grad_ref, curv_ref, grad_sum, curv_sum):
    height, breadth = hess.shape
    grad_ref[...] = grad.astype(grad_ref.dtype)
    grad_sum[...] += jnp.sum(grad * grad, axis=0, keepdims=True)
    same = same_block()
    size = jnp.abs(sign.astype(F32) * hess).astype(BF)
    for left in range(0, breadth, 256):
        wide = min(256, breadth - left)
        lanes = slice(left, left + wide)
        total = curv_sum[:, lanes]
        for top in range(0, height, 256):
            tall = min(256, height - top)
            sums = jnp.dot(
                same[:tall, :tall], size[top : top + tall, lanes], preferred_element_type=F32
            )
            means = jnp.dot(
                (sums * 0.0625).astype(BF), same[:wide, :wide], preferred_element_type=F32
            )
            curv_ref[top : top + tall, lanes] = means.astype(curv_ref.dtype)
            total = total + jnp.sum(means * means, axis=0, keepdims=True)
        curv_sum[:, lanes] = total


def pack_sums(grad_sum, curv_sum):
    lane = lax.broadcasted_iota(jnp.int32, (8, 128), 1)
    first = jnp.where(lane == 0, jnp.sum(grad_sum[...]), 0.0)
    return jnp.where(lane == 1, jnp.sum(curv_sum[...]), first)


def stacked(refs):
    return jnp.concatenate([r[...] for r in refs], axis=0)


def down_kernel(pieces, *refs):
    panel_ref, sign_ref = refs[:2]
    err_refs = refs[2 : 2 + pieces]
    dot_refs = refs[2 + pieces : 2 + 2 * pieces]
    grad_ref, curv_ref, pack_ref, grad_sum, curv_sum = refs[2 + 2 * pieces :]

    @pl.when(pl.program_id(0) == 0)
    def _():
        grad_sum[...] = jnp.zeros_like(grad_sum)
        curv_sum[...] = jnp.zeros_like(curv_sum)

    width = sign_ref.shape[0]
    err = stacked(err_refs)
    err_dot = stacked(dot_refs)
    plain = panel_ref[:width, :]
    grad = jnp.dot(plain, err, preferred_element_type=F32)
    hess = jnp.dot(panel_ref[width:, :], err, preferred_element_type=F32)
    hess = hess + jnp.dot(plain, err_dot, preferred_element_type=F32)
    finish_weight(grad, hess, sign_ref[...], grad_ref, curv_ref, grad_sum, curv_sum)

    @pl.when(pl.program_id(0) == pl.num_programs(0) - 1)
    def _():
        pack_ref[...] = pack_sums(grad_sum, curv_sum)


def down_grads(panel, sign, errs, dots):
    width, feats = sign.shape
    tile = side(feats)
    each = [cols_tile(errs[0].shape[0], tile)] * len(errs)
    return pl.pallas_call(
        lambda *refs: down_kernel(len(errs), *refs),
        grid=(feats // tile,),
        in_specs=[
            fixed(panel.shape), cols_tile(width, tile), *each, *each
        ],
        out_specs=[cols_tile(width, tile), cols_tile(width, tile), fixed((8, 128))],
        out_shape=[
            jax.ShapeDtypeStruct((width, feats), BF),
            jax.ShapeDtypeStruct((width, feats), BF),
            jax.ShapeDtypeStruct((8, 128), F32),
        ],
        scratch_shapes=[pltpu.VMEM((1, tile), F32), pltpu.VMEM((1, tile), F32)],
        compiler_params=pltpu.CompilerParams(dimension_semantics=("arbitrary",)),
        cost_estimate=pl.CostEstimate(
            flops=6 * width * feats * panel.shape[1], transcendentals=0, bytes_accessed=12 * width * feats
        ),
        name="down_grads",
    )(panel, sign, *errs, *dots)


def cotangents(d_refs, by_refs, cot_ref):
    width = d_refs[0].shape[0] // 2
    chunk = 16 if width % 16 == 0 else width

    def step(i, carry):
        def at(ref, n):
            return ref[pl.ds(pl.multiple_of(n * width + i * chunk, chunk), chunk), :].astype(F32)

        for shard, (d_ref, by_ref) in enumerate(zip(d_refs, by_refs)):
            count = d_ref.shape[1]
            d_hidden, d_hidden_dot = at(d_ref, 0), at(d_ref, 1)
            for_gate, for_up = at(by_ref, 0), at(by_ref, 1)
            for n, value in enumerate(
                (
                    d_hidden * for_gate,
                    d_hidden * for_up,
                    d_hidden_dot * for_gate + d_hidden * at(by_ref, 2),
                    d_hidden_dot * for_up + d_hidden * at(by_ref, 3),
                )
            ):
                rows = pl.ds(pl.multiple_of(n * width + i * chunk, chunk), chunk)
                cot_ref[rows, shard * count : (shard + 1) * count] = value.astype(BF)
        return carry

    lax.fori_loop(0, width // chunk, step, 0)


def wide_kernel(shards, *refs):
    sign_gate_ref, sign_up_ref, before_ref = refs[:3]
    token_refs, d_refs, by_refs = (refs[3 + n * shards : 3 + (n + 1) * shards] for n in range(3))
    grad_gate_ref, curv_gate_ref, grad_up_ref, curv_up_ref, pack_ref, grad_sum, curv_sum, cot_ref = refs[
        3 + 3 * shards :
    ]

    @pl.when(pl.program_id(0) == 0)
    def _():
        grad_sum[...] = jnp.zeros_like(grad_sum)
        curv_sum[...] = jnp.zeros_like(curv_sum)
        cotangents(d_refs, by_refs, cot_ref)

    width = sign_gate_ref.shape[0]
    tokens = stacked(token_refs)

    def product(at):
        return jnp.dot(cot_ref[at * width : (at + 1) * width, :], tokens, preferred_element_type=F32)

    finish_weight(
        product(0), product(2), sign_gate_ref[...], grad_gate_ref, curv_gate_ref, grad_sum, curv_sum
    )
    finish_weight(product(1), product(3), sign_up_ref[...], grad_up_ref, curv_up_ref, grad_sum, curv_sum)

    @pl.when(pl.program_id(0) == pl.num_programs(0) - 1)
    def _():
        pack_ref[...] = before_ref[...] + pack_sums(grad_sum, curv_sum)


def wide_grads(weights, before, tokens, ds, bys):
    feats = weights.shape[1]
    width = weights.shape[0] // 4
    tile = side(feats, 256)
    out = cols_tile(width, tile)
    count = tokens[0].shape[0] * len(tokens)
    return pl.pallas_call(
        lambda *refs: wide_kernel(len(tokens), *refs),
        grid=(feats // tile,),
        in_specs=[
            pl.BlockSpec((width, tile), lambda i: (2, i)),
            pl.BlockSpec((width, tile), lambda i: (3, i)),
            fixed((8, 128)),
            *[cols_tile(t.shape[0], tile) for t in tokens],
            *[fixed(d.shape) for d in ds],
            *[fixed(b.shape) for b in bys],
        ],
        out_specs=[out, out, out, out, fixed((8, 128))],
        out_shape=[jax.ShapeDtypeStruct((width, feats), BF)] * 4 + [jax.ShapeDtypeStruct((8, 128), F32)],
        scratch_shapes=[
            pltpu.VMEM((1, tile), F32), pltpu.VMEM((1, tile), F32), pltpu.VMEM((4 * width, count), BF)
        ],
        compiler_params=pltpu.CompilerParams(dimension_semantics=("arbitrary",)),
        cost_estimate=pl.CostEstimate(
            flops=8 * width * feats * count, transcendentals=0, bytes_accessed=20 * width * feats
        ),
        name="wide_grads",
    )(weights, weights, before, *tokens, *ds, *bys)


def update_kernel(scale_ref, *refs):
    fix_first = 1.0 - 0.9**STEP
    fix_second = 1.0 - 0.95**STEP
    by_grad = scale_ref[0]
    by_curv = scale_ref[1]
    for at in range(3):
        grad, curv, first, second = (refs[4 * at + n][...].astype(F32) for n in range(4))
        first_ref, second_ref, update_ref = (refs[12 + 3 * n + at] for n in range(3))
        new_first = 0.9 * first + 0.1 * (grad * by_grad)
        scaled = curv * by_curv
        new_second = 0.95 * second + 0.05 * (scaled * scaled)
        first_ref[...] = new_first
        second_ref[...] = new_second
        update_ref[...] = new_first * (1.0 / fix_first) / (jnp.sqrt(new_second * (1.0 / fix_second)) + 1e-08)


def update(scales, weights):
    width, feats = weights[0][0].shape
    tall = cols_tile(width, 128)
    shapes = [jax.ShapeDtypeStruct(w[0].shape, F32) for w in weights]
    return pl.pallas_call(
        update_kernel,
        grid=(feats // 128,),
        in_specs=[pl.BlockSpec(memory_space=pltpu.SMEM)] + [tall] * 12,
        out_specs=[tall] * 9,
        out_shape=shapes * 3,
        name="update",
    )(scales, *weights[0], *weights[1], *weights[2])


def activation(pre):
    sig = jax.nn.sigmoid(pre)
    act = pre * sig
    slope = sig * (1.0 + pre * (1.0 - sig))
    bend = sig * (1.0 - sig) * (2.0 + pre * (1.0 - 2.0 * sig))
    return (act, slope, bend)


def make_body(n_row, n_col):
    outer = n_row // 2
    rings = n_col // 2
    groups = rings // outer
    if n_row % 2 or n_col % 2 or rings % outer:
        raise ValueError("mesh")

    def pass_on(k, current):
        other = pair_swap(current, "col", n_col)
        if k > 0:
            following = ring_up(current, "col", n_col) if k < rings - 1 else None
            return following, current, other
        following = ring_up_apart(current, n_row, n_col) if rings > 1 else None
        core = lax.axis_index("row") % 2
        keep = jnp.where(core == 0, current, other)
        return following, keep, jnp.where(core == 0, other, current)

    def body(
        tokens, target, gate_weight, up_weight, down_weight, probe_gate, probe_up, probe_down,
        first_gate, first_up, first_down, second_gate, second_up, second_down,
    ):
        row = lax.axis_index("row")
        core = row % 2
        chip = row // 2
        gate_weight, up_weight, probe_gate, probe_up, first_gate, first_up, second_gate, second_up = (
            v.T
            for v in (
                gate_weight, up_weight, probe_gate, probe_up, first_gate, first_up, second_gate, second_up
            )
        )
        width, feats = gate_weight.shape
        count = tokens.shape[0]
        wide_weights, sign_down = signs(gate_weight, up_weight, probe_gate, probe_up, probe_down)

        token_shards = []
        pre_keeps = []
        current = tokens
        for k in range(rings):
            current, keep, send = pass_on(k, current)
            token_shards += [keep, send]
            both = dot(wide_weights, jnp.concatenate([send, keep], axis=0), (1, 1))
            sent = both[:, :count].astype(BF)
            pre_keeps.append(both[:, count:] + pair_swap(sent, "row", n_row).astype(F32))

        hidden_keeps = []
        hidden_sends = []
        owned = []
        for g in range(groups):
            mine = pre_keeps[g * outer : (g + 1) * outer]
            current = pick(mine, (chip - 1) % outer)
            for s in range(1, outer):
                got = ring_up(current.astype(BF), "row", n_row)
                current = got.astype(F32) + pick(mine, (chip - s - 1) % outer)
            pre_gate = current[:width]
            pre_up = current[width : 2 * width]
            dot_gate = current[2 * width : 3 * width]
            dot_up = current[3 * width :]
            act, slope, bend = activation(pre_gate)
            owned.append(
                jnp.concatenate(
                    [
                        (pre_up * slope).astype(BF),
                        act.astype(BF),
                        (dot_up * slope + pre_up * bend * dot_gate).astype(BF),
                        (slope * dot_gate).astype(BF),
                    ],
                    axis=0,
                )
            )
            hidden = (act * pre_up).astype(BF)
            hidden_dot = (slope * dot_gate * pre_up + act * dot_up).astype(BF)
            keeps = by_owner(gather_blocks(jnp.concatenate([hidden, hidden_dot], axis=0)), chip)
            both = jnp.concatenate(keeps, axis=1)
            sends = pair_swap(both, "row", n_row)
            hidden_keeps.append(both)
            hidden_sends.append(sends)

        near = ([], [])
        far = ([], [])
        for g in range(groups):
            sides = []
            for panel in (hidden_keeps[g], hidden_sends[g]):
                value = dot(panel[:width], down_weight, (0, 0))
                along = dot(panel[width:], down_weight, (0, 0)) + dot(panel[:width], sign_down, (0, 0))
                sides.append((value, along))
            for j in range(outer):
                for part in range(2):
                    own = sides[0][part][j * count : (j + 1) * count]
                    alien = sides[1][part][j * count : (j + 1) * count]
                    near[part].append(jnp.where(core == 0, own, alien))
                    far[part].append(jnp.where(core == 0, alien, own).astype(BF))
        order = [*range(1, rings), 0]
        reduced = {}
        for k in order:
            for part in range(2):
                reduced[k, part] = near[part][k] + pair_swap(far[part][k], "col", n_col).astype(F32)
        outputs = [reduced[order[0], part] for part in range(2)]
        for k in order[1:]:
            for part in range(2):
                moved = ring_up(outputs[part].astype(BF), "col", n_col)
                outputs[part] = moved.astype(F32) + reduced[k, part]
        errors = [(outputs[0] - target.astype(F32)).astype(BF), outputs[1].astype(BF)]

        error_shards = ([], [])
        ds = []
        bys = []
        for k in range(rings):
            if k == min(1, rings - 1):
                for g in range(groups):
                    got = gather_blocks(owned[g])
                    errors[0], *got = lax.optimization_barrier((errors[0], *got))
                    for keeps in by_owner(got, chip):
                        bys += [keeps, pair_swap(keeps, "row", n_row)]
            for part in range(2):
                errors[part], keep, send = pass_on(k, errors[part])
                error_shards[part].extend([keep, send])

            def term(at):
                err, err_dot = error_shards[0][2 * k + at], error_shards[1][2 * k + at]
                plain = dot(down_weight, err, (1, 1))
                along = dot(down_weight, err_dot, (1, 1)) + dot(sign_down, err, (1, 1))
                return plain, along

            sent = jnp.concatenate([v.astype(BF) for v in term(1)], axis=0)
            kept = jnp.concatenate(term(0), axis=0)
            total = kept + pair_swap(sent, "row", n_row).astype(F32)
            moving = total.astype(BF)
            for _ in range(1, outer):
                moving = ring_up(moving, "row", n_row)
                total = total + moving.astype(F32)
            keep_d = total.astype(BF)
            ds += [keep_d, pair_swap(keep_d, "row", n_row)]

        lanes = []
        for g in range(groups):
            for j in range(outer):
                lanes.append(hidden_keeps[g][:, j * count : (j + 1) * count])
                lanes.append(hidden_sends[g][:, j * count : (j + 1) * count])
        panel = jnp.concatenate(lanes, axis=1)
        grad_down, curv_down, partial = down_grads(panel, sign_down, *error_shards)
        grad_gate, curv_gate, grad_up, curv_up, packed = wide_grads(
            wide_weights, partial, token_shards, ds, bys
        )
        packed = total_over_all(packed, (("row", n_row), ("col", n_col)))
        entries = 3.0 * feats * n_row * width * n_col
        scales = 1.0 / jnp.sqrt(packed[0, :2] / entries + 1e-06)
        results = update(
            scales,
            (
                (grad_gate, curv_gate, first_gate, second_gate),
                (grad_up, curv_up, first_up, second_up),
                (grad_down, curv_down, first_down, second_down),
            ),
        )
        return tuple(v if i % 3 == 2 else v.T for i, v in enumerate(results))

    def gather_blocks(block):
        got = [block]
        for _ in range(1, outer):
            got.append(ring_up(got[-1], "row", n_row))
        return got

    def by_owner(got, chip):
        return [pick(got, (chip - j) % outer) for j in range(outer)]

    return body


def solution(mesh):
    wide = P("row", "col")
    tall = P("col", "row")
    inner = make_body(mesh.shape["row"], mesh.shape["col"])

    return jax.shard_map(
        inner,
        mesh=mesh,
        in_specs=(tall, tall, wide, wide, tall, wide, wide, tall, wide, wide, tall, wide, wide, tall),
        out_specs=(wide, wide, tall, wide, wide, tall, wide, wide, tall),
        check_vma=False,
    )
```

time: 387 us -> 381 us (0.984)
  Pallas kernels: 66.4 us -> 54.5 us
  waiting for transfers between devices: 227 us -> 234 us
  matrix products: 24.8 us -> 29.7 us
    ppermute x25 -> x22, waiting for transfers between devices: 136 us -> 151 us  [ring_up(): return lax.ppermute(value, axis, [(i, (i + 2) % size) for i in range(size)])]
    pallas_call x5 -> x1, Pallas kernels: 18.5 us -> 7.4 us  [signs(): pl.pallas_call(sign_kernel, grid=(feats // tile,), in_specs=[cols_tile(wi...]
    ppermute x38, waiting for transfers between devices: 76.1 us -> 65.2 us  [pair_swap(): return lax.ppermute(value, axis, [(i, i ^ 1) for i in range(size)])]
    ppermute x25 -> x22, starting transfers between devices: 17.6 us -> 11.7 us  [ring_up(): return lax.ppermute(value, axis, [(i, (i + 2) % size) for i in range(size)])]
    dot_general x40, matrix products: 24.8 us -> 29.7 us  [dot(): lax.dot_general(left, right, (((inner[0],), (inner[1],)), ((), ())), pref...]
  transfers between devices with their start and end apart: 68 -> 68, of which waited for: 40 -> 39; matrix products, arithmetic and copies ran while one was open for 9% -> 11% of each run, Pallas kernels for 7% -> 5%
where the time goes in v2:
time: 381 us; the launch traced here: 378 us
  waiting for transfers between devices  234 us (61%)
  Pallas kernels  54.5 us (14%)
  starting transfers between devices  41.7 us (11%)
  matrix products  29.7 us (8%)
  other arithmetic  10.6 us (3%)
  local copies, waits for them, and re-layouts  5.35 us (1%)
    ppermute x22, waiting for transfers between devices, ring_up(): return lax.ppermute(value, axis, [(i, (i + 2) % size) for i in range(size)])  151 us
    ppermute x38, waiting for transfers between devices, pair_swap(): return lax.ppermute(value, axis, [(i, i ^ 1) for i in range(size)])  65.2 us
    dot_general x40, matrix products, dot(): lax.dot_general(left, right, (((inner[0],), (inner[1],)), ((), ())), pref...  29.7 us
    ppermute x38, starting transfers between devices, pair_swap(): return lax.ppermute(value, axis, [(i, i ^ 1) for i in range(size)])  24.7 us
    pallas_call x1, Pallas kernels, update(): pl.pallas_call(update_kernel, grid=(feats // 128,), in_specs=[pl.BlockSpe...  20.3 us
    pallas_call x1, Pallas kernels, wide_grads(): pl.pallas_call(lambda *refs: wide_kernel(len(tokens), *refs), grid=(feats...  16.9 us
    ppermute x5, waiting for transfers between devices, total_over_all(): lax.ppermute(value, axis, [(i, i ^ step) for i in range(size)])  14.7 us
    ppermute x22, starting transfers between devices, ring_up(): return lax.ppermute(value, axis, [(i, (i + 2) % size) for i in range(size)])  11.7 us
  transfers between devices with their start and end apart: 68, of which 39 were waited for; matrix products, arithmetic and copies ran while one was open for 11% of the time, Pallas kernels for 5%

profile of v2, /device:TPU:0, one launch (start us, length us, event | category | flops | bytes accessed | tf_op | source)
XLA Modules:
  0.0 377.8 jit_solution(16222991488263587845)
XLA Ops:
  0.7 3.1 collective-permute-start
  3.8 1.5 collective-permute-start.3
  5.3 7.4 %signs.1 = (bf16[2752,1024]{1,0:T(8,128)(2,1)}, bf16[688,1024]{1,0:T(8,128)(2,1)}) custom-call(bf16[688,1024]{1,0:T(8,128)(2,1)} %bitcast.144, bf16[688,1024]{1,0:T(8,128)(2,1)} %bitcast.145, s32[688,1024]{1,0:T(8,128)} %bitcast.138, s32[688,1024]{1,0:T(8,128)} %bitcast.139, s32[688,1024]{1,0:T(8,128)} %probe_down_ref.1), custom_call_target="tpu_custom_call" | custom-call | tf_op jit(solution)/shard_map/signs/pallas_call | solution.py:79
  13.1 1.2 collective-permute-start.8
  15.6 4.6 %fusion.20 = f32[2752,256]{1,0:T(8,128)S(1)} fusion(bf16[2752,1024]{1,0:T(8,128)(2,1)} %get-tuple-element.34.refs_0_.refs_1_, bf16[128,1024]{1,0:T(8,128)(2,1)S(1)} %get-tuple-element.94.refs_3_, bf16[128,1024]{1,0:T(8,128)(2,1)S(1)} %get-tuple-element.93.refs_4_), kind=kOutput, calls=%fused_computation.76 | convolution fusion | flops 1443889152 | bytes 8978432 | tf_op jit(solution)/shard_map/dot_general | solution.py:15
  20.4 1.7 collective-permute-done.8.refs_7_
  22.1 2.5 collective-permute-start.12
  25.1 1.7 fusion.16
  27.0 7.6 %collective-permute-done.9.refs_9_ = bf16[128,1024]{1,0:T(8,128)(2,1)S(1)} collective-permute-done((bf16[128,1024]{1,0:T(8,128)(2,1)S(1)}, bf16[128,1024]{1,0:T(8,128)(2,1)S(1)}, u32[]{:S(2)}, u32[]{:S(2)}) %collective-permute-start.9) | collective-permute-done | bytes 262176 | tf_op jit(solution)/shard_map/ppermute | solution.py:30
  34.8 1.7 fusion.28
  36.8 4.7 %collective-permute-done.10.refs_10_ = bf16[128,1024]{1,0:T(8,128)(2,1)S(1)} collective-permute-done((bf16[128,1024]{1,0:T(8,128)(2,1)S(1)}, bf16[128,1024]{1,0:T(8,128)(2,1)S(1)}, u32[]{:S(2)}, u32[]{:S(2)}) %collective-permute-start.10) | collective-permute-done | bytes 262176 | tf_op jit(solution)/shard_map/ppermute | solution.py:26
  41.5 1.7 fusion.24
  44.5 1.0 collective-permute-done.11
  46.6 15.8 %collective-permute-done.5 = bf16[2752,128]{1,0:T(8,128)(2,1)S(1)} collective-permute-done((bf16[2752,128]{1,0:T(8,128)(2,1)S(1)}, bf16[2752,128]{1,0:T(8,128)(2,1)S(1)}, u32[]{:S(2)}, u32[]{:S(2)}) %collective-permute-start.5) | collective-permute-done | bytes 704544 | tf_op jit(solution)/shard_map/ppermute | solution.py:30
  64.0 1.3 collective-permute-start.26
  65.3 19.7 %collective-permute-done.6 = bf16[1376,128]{1,0:T(8,128)(2,1)S(1)} collective-permute-done((bf16[1376,128]{1,0:T(8,128)(2,1)S(1)}, bf16[1376,128]{1,0:T(8,128)(2,1)S(1)}, u32[]{:S(2)}, u32[]{:S(2)}) %collective-permute-start.6) | collective-permute-done | bytes 352288 | tf_op jit(solution)/shard_map/ppermute | solution.py:30
  89.5 1.3 collective-permute-start.27
  91.2 16.5 %collective-permute-done.15 = bf16[1376,128]{1,0:T(8,128)(2,1)S(1)} collective-permute-done((bf16[1376,128]{1,0:T(8,128)(2,1)S(1)}, bf16[1376,128]{1,0:T(8,128)(2,1)S(1)}, u32[]{:S(2)}, u32[]{:S(2)}) %collective-permute-start.15) | collective-permute-done | bytes 352288 | tf_op jit(solution)/shard_map/ppermute | solution.py:30
  110.6 1.5 collective-permute-start.23
  114.1 5.1 %collective-permute-done.17 = bf16[128,1024]{1,0:T(8,128)(2,1)S(1)} collective-permute-done((bf16[128,1024]{1,0:T(8,128)(2,1)S(1)}, bf16[128,1024]{1,0:T(8,128)(2,1)S(1)}, u32[]{:S(2)}, u32[]{:S(2)}) %collective-permute-start.17) | collective-permute-done | bytes 262176 | tf_op jit(solution)/shard_map/ppermute | solution.py:26
  119.9 10.1 %collective-permute-done.33 = bf16[128,1024]{1,0:T(8,128)(2,1)S(1)} collective-permute-done((bf16[128,1024]{1,0:T(8,128)(2,1)S(1)}, bf16[128,1024]{1,0:T(8,128)(2,1)S(1)}, u32[]{:S(2)}, u32[]{:S(2)}) %collective-permute-start.33) | collective-permute-done | bytes 262176 | tf_op jit(solution)/shard_map/ppermute | solution.py:26
  133.0 0.9 copy-done.37
  134.1 5.6 %collective-permute-done.18 = bf16[128,1024]{1,0:T(8,128)(2,1)S(1)} collective-permute-done((bf16[128,1024]{1,0:T(8,128)(2,1)S(1)}, bf16[128,1024]{1,0:T(8,128)(2,1)S(1)}, u32[]{:S(2)}, u32[]{:S(2)}) %collective-permute-start.18) | collective-permute-done | bytes 262176 | tf_op jit(solution)/shard_map/ppermute | solution.py:30
  140.4 8.1 %collective-permute-done.34 = bf16[128,1024]{1,0:T(8,128)(2,1)S(1)} collective-permute-done((bf16[128,1024]{1,0:T(8,128)(2,1)S(1)}, bf16[128,1024]{1,0:T(8,128)(2,1)S(1)}, u32[]{:S(2)}, u32[]{:S(2)}) %collective-permute-start.34) | collective-permute-done | bytes 262176 | tf_op jit(solution)/shard_map/ppermute | solution.py:30
  149.1 6.3 %collective-permute-done.21 = bf16[128,1024]{1,0:T(8,128)(2,1)S(1)} collective-permute-done((bf16[128,1024]{1,0:T(8,128)(2,1)S(1)}, bf16[128,1024]{1,0:T(8,128)(2,1)S(1)}, u32[]{:S(2)}, u32[]{:S(2)}) %collective-permute-start.21) | collective-permute-done | bytes 262176 | tf_op jit(solution)/shard_map/ppermute | solution.py:26
  156.0 1.2 collective-permute-done.20
  157.3 6.3 %collective-permute-done.37 = bf16[128,1024]{1,0:T(8,128)(2,1)S(1)} collective-permute-done((bf16[128,1024]{1,0:T(8,128)(2,1)S(1)}, bf16[128,1024]{1,0:T(8,128)(2,1)S(1)}, u32[]{:S(2)}, u32[]{:S(2)}) %collective-permute-start.37) | collective-permute-done | bytes 262176 | tf_op jit(solution)/shard_map/ppermute | solution.py:26
  163.8 1.7 collective-permute-done.36
  166.6 7.5 %collective-permute-done.22 = bf16[128,1024]{1,0:T(8,128)(2,1)S(1)} collective-permute-done((bf16[128,1024]{1,0:T(8,128)(2,1)S(1)}, bf16[128,1024]{1,0:T(8,128)(2,1)S(1)}, u32[]{:S(2)}, u32[]{:S(2)}) %collective-permute-start.22) | collective-permute-done | bytes 262176 | tf_op jit(solution)/shard_map/ppermute | solution.py:30
  174.3 2.5 collective-permute-start.24
  176.7 2.9 collective-permute-done.38
  179.9 2.5 collective-permute-start.40
  182.3 2.9 collective-permute-done.25.refs_4_
  185.3 2.5 collective-permute-start.28
  189.6 1.1 broadcast_select_fusion.3
  197.5 7.2 %collective-permute-done.42.refs_13_ = bf16[128,1024]{1,0:T(8,128)(2,1)S(1)} collective-permute-done((bf16[128,1024]{1,0:T(8,128)(2,1)S(1)}, bf16[128,1024]{1,0:T(8,128)(2,1)S(1)}, u32[]{:S(2)}, u32[]{:S(2)}) %collective-permute-start.42) | collective-permute-done | bytes 262176 | tf_op jit(solution)/shard_map/ppermute | solution.py:26
  206.1 8.4 %collective-permute-done.43.refs_14_ = bf16[128,1024]{1,0:T(8,128)(2,1)S(1)} collective-permute-done((bf16[128,1024]{1,0:T(8,128)(2,1)S(1)}, bf16[128,1024]{1,0:T(8,128)(2,1)S(1)}, u32[]{:S(2)}, u32[]{:S(2)}) %collective-permute-start.43) | collective-permute-done | bytes 262176 | tf_op jit(solution)/shard_map/ppermute | solution.py:30
  215.2 10.4 %collective-permute-done.31.refs_8_ = bf16[128,1024]{1,0:T(8,128)(2,1)S(1)} collective-permute-done((bf16[128,1024]{1,0:T(8,128)(2,1)S(1)}, bf16[128,1024]{1,0:T(8,128)(2,1)S(1)}, u32[]{:S(2)}, u32[]{:S(2)}) %collective-permute-start.31) | collective-permute-done | bytes 262176 | tf_op jit(solution)/shard_map/ppermute | solution.py:30
  225.6 1.1 collective-permute-start.30
  227.8 5.7 %collective-permute-done.30.refs_7_ = bf16[128,1024]{1,0:T(8,128)(2,1)S(1)} collective-permute-done((bf16[128,1024]{1,0:T(8,128)(2,1)S(1)}, bf16[128,1024]{1,0:T(8,128)(2,1)S(1)}, u32[]{:S(2)}, u32[]{:S(2)}) %collective-permute-start.30) | collective-permute-done | bytes 262176 | tf_op jit(solution)/shard_map/ppermute | solution.py:26
  233.5 1.1 collective-permute-start.44
  235.1 5.4 %collective-permute-done.44.refs_15_ = bf16[128,1024]{1,0:T(8,128)(2,1)S(1)} collective-permute-done((bf16[128,1024]{1,0:T(8,128)(2,1)S(1)}, bf16[128,1024]{1,0:T(8,128)(2,1)S(1)}, u32[]{:S(2)}, u32[]{:S(2)}) %collective-permute-start.44) | collective-permute-done | bytes 262176 | tf_op jit(solution)/shard_map/ppermute | solution.py:26
  241.6 7.0 %collective-permute-done.45.refs_16_ = bf16[128,1024]{1,0:T(8,128)(2,1)S(1)} collective-permute-done((bf16[128,1024]{1,0:T(8,128)(2,1)S(1)}, bf16[128,1024]{1,0:T(8,128)(2,1)S(1)}, u32[]{:S(2)}, u32[]{:S(2)}) %collective-permute-start.45) | collective-permute-done | bytes 262176 | tf_op jit(solution)/shard_map/ppermute | solution.py:30
  250.1 9.8 %collective-permute-done.48 = bf16[1376,128]{1,0:T(8,128)(2,1)S(1)} collective-permute-done((bf16[1376,128]{1,0:T(8,128)(2,1)S(1)}, bf16[1376,128]{1,0:T(8,128)(2,1)S(1)}, u32[]{:S(2)}, u32[]{:S(2)}) %collective-permute-start.48) | collective-permute-done | bytes 352288 | tf_op jit(solution)/shard_map/ppermute | solution.py:30
  260.0 1.1 collective-permute-start.32
  261.0 0.9 add_convert_fusion.3.refs_11_
  261.9 5.9 %collective-permute-done.32.refs_9_ = bf16[128,1024]{1,0:T(8,128)(2,1)S(1)} collective-permute-done((bf16[128,1024]{1,0:T(8,128)(2,1)S(1)}, bf16[128,1024]{1,0:T(8,128)(2,1)S(1)}, u32[]{:S(2)}, u32[]{:S(2)}) %collective-permute-start.32) | collective-permute-done | bytes 262176 | tf_op jit(solution)/shard_map/ppermute | solution.py:26
  267.8 1.1 collective-permute-start.46
  269.4 5.4 %collective-permute-done.46.refs_17_ = bf16[128,1024]{1,0:T(8,128)(2,1)S(1)} collective-permute-done((bf16[128,1024]{1,0:T(8,128)(2,1)S(1)}, bf16[128,1024]{1,0:T(8,128)(2,1)S(1)}, u32[]{:S(2)}, u32[]{:S(2)}) %collective-permute-start.46) | collective-permute-done | bytes 262176 | tf_op jit(solution)/shard_map/ppermute | solution.py:26
  277.3 9.5 %collective-permute-done.51 = bf16[1376,128]{1,0:T(8,128)(2,1)S(1)} collective-permute-done((bf16[1376,128]{1,0:T(8,128)(2,1)S(1)}, bf16[1376,128]{1,0:T(8,128)(2,1)S(1)}, u32[]{:S(2)}, u32[]{:S(2)}) %collective-permute-start.51) | collective-permute-done | bytes 352288 | tf_op jit(solution)/shard_map/ppermute | solution.py:30
  286.8 0.9 add_convert_fusion.2.refs_13_
  289.2 9.5 %collective-permute-done.54 = bf16[1376,128]{1,0:T(8,128)(2,1)S(1)} collective-permute-done((bf16[1376,128]{1,0:T(8,128)(2,1)S(1)}, bf16[1376,128]{1,0:T(8,128)(2,1)S(1)}, u32[]{:S(2)}, u32[]{:S(2)}) %collective-permute-start.54) | collective-permute-done | bytes 352288 | tf_op jit(solution)/shard_map/ppermute | solution.py:30
  299.4 0.9 add_convert_fusion.1.refs_15_
  300.3 7.8 %collective-permute-done.57 = bf16[1376,128]{1,0:T(8,128)(2,1)S(1)} collective-permute-done((bf16[1376,128]{1,0:T(8,128)(2,1)S(1)}, bf16[1376,128]{1,0:T(8,128)(2,1)S(1)}, u32[]{:S(2)}, u32[]{:S(2)}) %collective-permute-start.57) | collective-permute-done | bytes 352288 | tf_op jit(solution)/shard_map/ppermute | solution.py:30
  308.1 0.9 add_convert_fusion.refs_17_
  311.5 9.9 %down_grads.1 = (bf16[688,1024]{1,0:T(8,128)(2,1)}, bf16[688,1024]{1,0:T(8,128)(2,1)}, f32[8,128]{1,0:T(8,128)}) custom-call(bf16[1376,1024]{1,0:T(8,128)(2,1)} %copy-done.37, bf16[688,1024]{1,0:T(8,128)(2,1)} %get-tuple-element.35.refs_1_, bf16[128,1024]{1,0:T(8,128)(2,1)} %copy-done.6, bf16[128,1024]{1,0:T(8,128)(2,1)} %copy-done.5, ...), custom_call_target="tpu_custom_call" | custom-call | flops 4328521728 | bytes 8454144 | tf_op jit(solution)/shard_map/down_grads/pallas_call | solution.py:157
  322.4 16.9 %wide_grads.1 = (bf16[688,1024]{1,0:T(8,128)(2,1)}, bf16[688,1024]{1,0:T(8,128)(2,1)}, bf16[688,1024]{1,0:T(8,128)(2,1)}, bf16[688,1024]{1,0:T(8,128)(2,1)}, f32[8,128]{1,0:T(8,128)}) custom-call(bf16[2752,1024]{1,0:T(8,128)(2,1)} %get-tuple-element.34.refs_0_.refs_1_, bf16[2752,1024]{1,0:T(8,128)(2,1)} %get-tuple-element.34.refs_0_.refs_1_, ...), custom_call_target="tpu_custom_call" | custom-call | flops 5771362304 | bytes 14090240 | tf_op jit(solution)/shard_map/wide_grads/pallas_call | solution.py:240
  339.6 1.1 collective-permute-done.63
  342.1 2.9 collective-permute-done.64
  345.0 1.0 collective-permute-start.65
  346.0 2.6 collective-permute-done.65
  348.6 3.6 collective-permute-done.66
  352.2 4.5 %collective-permute-done.67 = f32[8,128]{1,0:T(8,128)S(1)} collective-permute-done((f32[8,128]{1,0:T(8,128)S(1)}, f32[8,128]{1,0:T(8,128)S(1)}, u32[]{:S(2)}, u32[]{:S(2)}) %collective-permute-start.67) | collective-permute-done | bytes 4128 | tf_op jit(solution)/shard_map/ppermute | solution.py:46
  357.3 20.3 %update.1 = (f32[688,1024]{1,0:T(8,128)}, f32[688,1024]{1,0:T(8,128)}, f32[688,1024]{1,0:T(8,128)}, f32[688,1024]{1,0:T(8,128)}, f32[688,1024]{1,0:T(8,128)}, /*...) custom-call(f32[2]{0:T(128)} %rsqrt_bitcast_fusion.scale_ref, ...), custom_call_target="tpu_custom_call" | custom-call | tf_op jit(solution)/shard_map/update/pallas_call | solution.py:284
  (256 shorter events, 49.5 us)
Async XLA Ops:
  0.7 12.5 %collective-permute-start = (bf16[128,1024]{1,0:T(8,128)(2,1)}, bf16[128,1024]{1,0:T(8,128)(2,1)S(1)}, u32[]{:S(2)}, u32[]{:S(2)}) collective-permute-start(bf16[128,1024]{1,0:T(8,128)(2,1)} %param.14), channel_id=1, source_target_pairs={{0,2},{1,3},{2,4},{3,5},{4,6},{5,7},{6,0},{7,1},{8,11},{9,10},{10,... | collective-permute-start | bytes 786440 | tf_op jit(solution)/shard_map/ppermute | solution.py:38
  3.8 11.7 %collective-permute-start.3 = (bf16[128,1024]{1,0:T(8,128)(2,1)}, bf16[128,1024]{1,0:T(8,128)(2,1)S(1)}, u32[]{:S(2)}, u32[]{:S(2)}) collective-permute-start(bf16[128,1024]{1,0:T(8,128)(2,1)} %param.14), channel_id=1, source_target_pairs={{0,1},{1,0},{2,3},{3,2},{4,5},{5,4},{6,7},{7,6},{8,9},{9,8},{10,11... | collective-permute-start | bytes 786440 | tf_op jit(solution)/shard_map/ppermute | solution.py:26
  13.1 8.9 %collective-permute-start.8 = (bf16[128,1024]{1,0:T(8,128)(2,1)S(1)}, bf16[128,1024]{1,0:T(8,128)(2,1)S(1)}, u32[]{:S(2)}, u32[]{:S(2)}) collective-permute-start(bf16[128,1024]{1,0:T(8,128)(2,1)S(1)} %collective-permute-done.refs_5_), channel_id=1, source_target_pairs={{0,2},{1,3},{2,4},{3,5},{4,6},{5,7},{6,0},{7,1},{8,10},{9,11},{10,... | collective-permute-start | bytes 786440 | tf_op jit(solution)/shard_map/ppermute | solution.py:30
  14.3 10.7 %collective-permute-start.1 = (bf16[128,1024]{1,0:T(8,128)(2,1)S(1)}, bf16[128,1024]{1,0:T(8,128)(2,1)S(1)}, u32[]{:S(2)}, u32[]{:S(2)}) collective-permute-start(bf16[128,1024]{1,0:T(8,128)(2,1)S(1)} %collective-permute-done.refs_5_), channel_id=1, source_target_pairs={{0,1},{1,0},{2,3},{3,2},{4,5},{5,4},{6,7},{7,6},{8,9},{9,8},{10,11... | collective-permute-start | bytes 786440 | tf_op jit(solution)/shard_map/ppermute | solution.py:26
  20.3 23.1 %collective-permute-start.4 = (bf16[2752,128]{1,0:T(8,128)(2,1)S(1)}, bf16[2752,128]{1,0:T(8,128)(2,1)S(1)}, u32[]{:S(2)}, u32[]{:S(2)}) collective-permute-start(bf16[2752,128]{1,0:T(8,128)(2,1)S(1)} %slice.405), channel_id=1, source_target_pairs={{0,8},{8,0},{16,24},{24,16},{1,9},{9,1},{17,25},{25,17},{2,10},{10... | collective-permute-start | bytes 2113544 | tf_op jit(solution)/shard_map/ppermute | solution.py:26
  22.1 12.8 %collective-permute-start.12 = (bf16[128,1024]{1,0:T(8,128)(2,1)S(1)}, bf16[128,1024]{1,0:T(8,128)(2,1)S(1)}, u32[]{:S(2)}, u32[]{:S(2)}) collective-permute-start(bf16[128,1024]{1,0:T(8,128)(2,1)S(1)} %collective-permute-done.8.refs_7_), channel_id=1, source_target_pairs={{0,1},{1,0},{2,3},{3,2},{4,5},{5,4},{6,7},{7,6},{8,9},{9,8},{10,11... | collective-permute-start | bytes 786440 | tf_op jit(solution)/shard_map/ppermute | solution.py:26
  24.6 10.0 %collective-permute-start.9 = (bf16[128,1024]{1,0:T(8,128)(2,1)S(1)}, bf16[128,1024]{1,0:T(8,128)(2,1)S(1)}, u32[]{:S(2)}, u32[]{:S(2)}) collective-permute-start(bf16[128,1024]{1,0:T(8,128)(2,1)S(1)} %collective-permute-done.8.refs_7_), channel_id=1, source_target_pairs={{0,2},{1,3},{2,4},{3,5},{4,6},{5,7},{6,0},{7,1},{8,10},{9,11},{10,... | collective-permute-start | bytes 786440 | tf_op jit(solution)/shard_map/ppermute | solution.py:30
  26.9 16.5 %collective-permute-start.2 = (bf16[2752,128]{1,0:T(8,128)(2,1)S(1)}, bf16[2752,128]{1,0:T(8,128)(2,1)S(1)}, u32[]{:S(2)}, u32[]{:S(2)}) collective-permute-start(bf16[2752,128]{1,0:T(8,128)(2,1)S(1)} %slice.406), channel_id=1, source_target_pairs={{0,8},{8,0},{16,24},{24,16},{1,9},{9,1},{17,25},{25,17},{2,10},{10... | collective-permute-start | bytes 2113544 | tf_op jit(solution)/shard_map/ppermute | solution.py:26
  34.6 6.9 %collective-permute-start.10 = (bf16[128,1024]{1,0:T(8,128)(2,1)S(1)}, bf16[128,1024]{1,0:T(8,128)(2,1)S(1)}, u32[]{:S(2)}, u32[]{:S(2)}) collective-permute-start(bf16[128,1024]{1,0:T(8,128)(2,1)S(1)} %collective-permute-done.9.refs_9_), channel_id=1, source_target_pairs={{0,1},{1,0},{2,3},{3,2},{4,5},{5,4},{6,7},{7,6},{8,9},{9,8},{10,11... | collective-permute-start | bytes 786440 | tf_op jit(solution)/shard_map/ppermute | solution.py:26
  36.7 7.8 %collective-permute-start.13 = (bf16[2752,128]{1,0:T(8,128)(2,1)S(1)}, bf16[2752,128]{1,0:T(8,128)(2,1)S(1)}, u32[]{:S(2)}, u32[]{:S(2)}) collective-permute-start(bf16[2752,128]{1,0:T(8,128)(2,1)S(1)} %slice.403), channel_id=1, source_target_pairs={{0,8},{8,0},{16,24},{24,16},{1,9},{9,1},{17,25},{25,17},{2,10},{10... | collective-permute-start | bytes 2113544 | tf_op jit(solution)/shard_map/ppermute | solution.py:26
  43.7 18.7 %collective-permute-start.5 = (bf16[2752,128]{1,0:T(8,128)(2,1)S(1)}, bf16[2752,128]{1,0:T(8,128)(2,1)S(1)}, u32[]{:S(2)}, u32[]{:S(2)}) collective-permute-start(bf16[2752,128]{1,0:T(8,128)(2,1)S(1)} %select_convert_fusion.1), channel_id=1, source_target_pairs={{0,16},{8,24},{16,0},{24,8},{1,17},{9,25},{17,1},{25,9},{2,18},{10... | collective-permute-start | bytes 2113544 | tf_op jit(solution)/shard_map/ppermute | solution.py:30
  45.8 42.0 %collective-permute-start.14 = (bf16[2752,128]{1,0:T(8,128)(2,1)S(1)}, bf16[2752,128]{1,0:T(8,128)(2,1)S(1)}, u32[]{:S(2)}, u32[]{:S(2)}) collective-permute-start(bf16[2752,128]{1,0:T(8,128)(2,1)S(1)} %select_convert_fusion), channel_id=1, source_target_pairs={{0,16},{8,24},{16,0},{24,8},{1,17},{9,25},{17,1},{25,9},{2,18},{10... | collective-permute-start | bytes 2113544 | tf_op jit(solution)/shard_map/ppermute | solution.py:30
  63.1 21.9 %collective-permute-start.6 = (bf16[1376,128]{1,0:T(8,128)(2,1)S(1)}, bf16[1376,128]{1,0:T(8,128)(2,1)S(1)}, u32[]{:S(2)}, u32[]{:S(2)}) collective-permute-start(bf16[1376,128]{1,0:T(8,128)(2,1)S(1)} %pad_maximum_fusion.4), channel_id=1, source_target_pairs={{0,16},{8,24},{16,0},{24,8},{1,17},{9,25},{17,1},{25,9},{2,18},{10... | collective-permute-start | bytes 1056776 | tf_op jit(solution)/shard_map/ppermute | solution.py:30
  64.0 115.8 %collective-permute-start.26 = (bf16[2752,128]{1,0:T(8,128)(2,1)S(1)}, bf16[2752,128]{1,0:T(8,128)(2,1)S(1)}, u32[]{:S(2)}, u32[]{:S(2)}) collective-permute-start(bf16[2752,128]{1,0:T(8,128)(2,1)S(1)} %pad_maximum_fusion.2), channel_id=1, source_target_pairs={{0,16},{8,24},{16,0},{24,8},{1,17},{9,25},{17,1},{25,9},{2,18},{10... | collective-permute-start | bytes 2113544 | tf_op jit(solution)/shard_map/ppermute | solution.py:30
  85.3 5.5 %collective-permute-start.7 = (bf16[1376,256]{1,0:T(8,128)(2,1)S(1)}, bf16[1376,256]{1,0:T(8,128)(2,1)S(1)}, u32[]{:S(2)}, u32[]{:S(2)}) collective-permute-start(bf16[1376,256]{1,0:T(8,128)(2,1)S(1)} %pad_maximum_fusion), channel_id=1, source_target_pairs={{0,8},{8,0},{16,24},{24,16},{1,9},{9,1},{17,25},{25,17},{2,10},{10... | collective-permute-start | bytes 2113544 | tf_op jit(solution)/shard_map/ppermute | solution.py:26
  88.6 19.1 %collective-permute-start.15 = (bf16[1376,128]{1,0:T(8,128)(2,1)S(1)}, bf16[1376,128]{1,0:T(8,128)(2,1)S(1)}, u32[]{:S(2)}, u32[]{:S(2)}) collective-permute-start(bf16[1376,128]{1,0:T(8,128)(2,1)S(1)} %pad_maximum_fusion.5), channel_id=1, source_target_pairs={{0,16},{8,24},{16,0},{24,8},{1,17},{9,25},{17,1},{25,9},{2,18},{10... | collective-permute-start | bytes 1056776 | tf_op jit(solution)/shard_map/ppermute | solution.py:30
  89.5 95.8 %collective-permute-start.27 = (bf16[2752,128]{1,0:T(8,128)(2,1)S(1)}, bf16[2752,128]{1,0:T(8,128)(2,1)S(1)}, u32[]{:S(2)}, u32[]{:S(2)}) collective-permute-start(bf16[2752,128]{1,0:T(8,128)(2,1)S(1)} %pad_maximum_fusion.3), channel_id=1, source_target_pairs={{0,16},{8,24},{16,0},{24,8},{1,17},{9,25},{17,1},{25,9},{2,18},{10... | collective-permute-start | bytes 2113544 | tf_op jit(solution)/shard_map/ppermute | solution.py:30
  109.2 20.9 %collective-permute-start.16 = (bf16[1376,256]{1,0:T(8,128)(2,1)S(1)}, bf16[1376,256]{1,0:T(8,128)(2,1)S(1)}, u32[]{:S(2)}, u32[]{:S(2)}) collective-permute-start(bf16[1376,256]{1,0:T(8,128)(2,1)S(1)} %pad_maximum_fusion.1), channel_id=1, source_target_pairs={{0,8},{8,0},{16,24},{24,16},{1,9},{9,1},{17,25},{25,17},{2,10},{10... | collective-permute-start | bytes 2113544 | tf_op jit(solution)/shard_map/ppermute | solution.py:26
  110.0 9.2 %collective-permute-start.17 = (bf16[128,1024]{1,0:T(8,128)(2,1)S(1)}, bf16[128,1024]{1,0:T(8,128)(2,1)S(1)}, u32[]{:S(2)}, u32[]{:S(2)}) collective-permute-start(bf16[128,1024]{1,0:T(8,128)(2,1)S(1)} %get-tuple-element.67), channel_id=1, source_target_pairs={{0,1},{1,0},{2,3},{3,2},{4,5},{5,4},{6,7},{7,6},{8,9},{9,8},{10,11... | collective-permute-start | bytes 786440 | tf_op jit(solution)/shard_map/ppermute | solution.py:26
  110.6 55.1 %collective-permute-start.23 = (bf16[128,1024]{1,0:T(8,128)(2,1)S(1)}, bf16[128,1024]{1,0:T(8,128)(2,1)S(1)}, u32[]{:S(2)}, u32[]{:S(2)}) collective-permute-start(bf16[128,1024]{1,0:T(8,128)(2,1)S(1)} %get-tuple-element.68), channel_id=1, source_target_pairs={{0,1},{1,0},{2,3},{3,2},{4,5},{5,4},{6,7},{7,6},{8,9},{9,8},{10,11... | collective-permute-start | bytes 786440 | tf_op jit(solution)/shard_map/ppermute | solution.py:26
  119.2 10.8 %collective-permute-start.33 = (bf16[128,1024]{1,0:T(8,128)(2,1)S(1)}, bf16[128,1024]{1,0:T(8,128)(2,1)S(1)}, u32[]{:S(2)}, u32[]{:S(2)}) collective-permute-start(bf16[128,1024]{1,0:T(8,128)(2,1)S(1)} %get-tuple-element.63), channel_id=1, source_target_pairs={{0,1},{1,0},{2,3},{3,2},{4,5},{5,4},{6,7},{7,6},{8,9},{9,8},{10,11... | collective-permute-start | bytes 786440 | tf_op jit(solution)/shard_map/ppermute | solution.py:26
  130.0 9.7 %collective-permute-start.18 = (bf16[128,1024]{1,0:T(8,128)(2,1)S(1)}, bf16[128,1024]{1,0:T(8,128)(2,1)S(1)}, u32[]{:S(2)}, u32[]{:S(2)}) collective-permute-start(bf16[128,1024]{1,0:T(8,128)(2,1)S(1)} %add_convert_fusion.10), channel_id=1, source_target_pairs={{0,2},{1,3},{2,4},{3,5},{4,6},{5,7},{6,0},{7,1},{8,10},{9,11},{10,... | collective-permute-start | bytes 786440 | tf_op jit(solution)/shard_map/ppermute | solution.py:30
  131.1 8.6 %collective-permute-start.19 = (bf16[128,1024]{1,0:T(8,128)(2,1)S(1)}, bf16[128,1024]{1,0:T(8,128)(2,1)S(1)}, u32[]{:S(2)}, u32[]{:S(2)}) collective-permute-start(bf16[128,1024]{1,0:T(8,128)(2,1)S(1)} %get-tuple-element.69), channel_id=1, source_target_pairs={{0,1},{1,0},{2,3},{3,2},{4,5},{5,4},{6,7},{7,6},{8,9},{9,8},{10,11... | collective-permute-start | bytes 786440 | tf_op jit(solution)/shard_map/ppermute | solution.py:26
  139.6 8.8 %collective-permute-start.34 = (bf16[128,1024]{1,0:T(8,128)(2,1)S(1)}, bf16[128,1024]{1,0:T(8,128)(2,1)S(1)}, u32[]{:S(2)}, u32[]{:S(2)}) collective-permute-start(bf16[128,1024]{1,0:T(8,128)(2,1)S(1)} %add_convert_fusion.7), channel_id=1, source_target_pairs={{0,2},{1,3},{2,4},{3,5},{4,6},{5,7},{6,0},{7,1},{8,10},{9,11},{10,... | collective-permute-start | bytes 786440 | tf_op jit(solution)/shard_map/ppermute | solution.py:30
  139.6 9.3 %collective-permute-start.35 = (bf16[128,1024]{1,0:T(8,128)(2,1)S(1)}, bf16[128,1024]{1,0:T(8,128)(2,1)S(1)}, u32[]{:S(2)}, u32[]{:S(2)}) collective-permute-start(bf16[128,1024]{1,0:T(8,128)(2,1)S(1)} %get-tuple-element.65), channel_id=1, source_target_pairs={{0,1},{1,0},{2,3},{3,2},{4,5},{5,4},{6,7},{7,6},{8,9},{9,8},{10,11... | collective-permute-start | bytes 786440 | tf_op jit(solution)/shard_map/ppermute | solution.py:26
  148.4 7.0 %collective-permute-start.21 = (bf16[128,1024]{1,0:T(8,128)(2,1)S(1)}, bf16[128,1024]{1,0:T(8,128)(2,1)S(1)}, u32[]{:S(2)}, u32[]{:S(2)}) collective-permute-start(bf16[128,1024]{1,0:T(8,128)(2,1)S(1)} %get-tuple-element.70), channel_id=1, source_target_pairs={{0,1},{1,0},{2,3},{3,2},{4,5},{5,4},{6,7},{7,6},{8,9},{9,8},{10,11... | collective-permute-start | bytes 786440 | tf_op jit(solution)/shard_map/ppermute | solution.py:26
  149.0 8.2 %collective-permute-start.20 = (bf16[128,1024]{1,0:T(8,128)(2,1)S(1)}, bf16[128,1024]{1,0:T(8,128)(2,1)S(1)}, u32[]{:S(2)}, u32[]{:S(2)}) collective-permute-start(bf16[128,1024]{1,0:T(8,128)(2,1)S(1)} %add_convert_fusion.9), channel_id=1, source_target_pairs={{0,2},{1,3},{2,4},{3,5},{4,6},{5,7},{6,0},{7,1},{8,10},{9,11},{10,... | collective-permute-start | bytes 786440 | tf_op jit(solution)/shard_map/ppermute | solution.py:30
  155.4 8.1 %collective-permute-start.37 = (bf16[128,1024]{1,0:T(8,128)(2,1)S(1)}, bf16[128,1024]{1,0:T(8,128)(2,1)S(1)}, u32[]{:S(2)}, u32[]{:S(2)}) collective-permute-start(bf16[128,1024]{1,0:T(8,128)(2,1)S(1)} %get-tuple-element.66), channel_id=1, source_target_pairs={{0,1},{1,0},{2,3},{3,2},{4,5},{5,4},{6,7},{7,6},{8,9},{9,8},{10,11... | collective-permute-start | bytes 786440 | tf_op jit(solution)/shard_map/ppermute | solution.py:26
  157.2 8.4 %collective-permute-start.36 = (bf16[128,1024]{1,0:T(8,128)(2,1)S(1)}, bf16[128,1024]{1,0:T(8,128)(2,1)S(1)}, u32[]{:S(2)}, u32[]{:S(2)}) collective-permute-start(bf16[128,1024]{1,0:T(8,128)(2,1)S(1)} %add_convert_fusion.6), channel_id=1, source_target_pairs={{0,2},{1,3},{2,4},{3,5},{4,6},{5,7},{6,0},{7,1},{8,10},{9,11},{10,... | collective-permute-start | bytes 786440 | tf_op jit(solution)/shard_map/ppermute | solution.py:30
  163.6 10.7 %collective-permute-start.39 = (bf16[128,1024]{1,0:T(8,128)(2,1)S(1)}, bf16[128,1024]{1,0:T(8,128)(2,1)S(1)}, u32[]{:S(2)}, u32[]{:S(2)}) collective-permute-start(bf16[128,1024]{1,0:T(8,128)(2,1)S(1)} %get-tuple-element.64), channel_id=1, source_target_pairs={{0,1},{1,0},{2,3},{3,2},{4,5},{5,4},{6,7},{7,6},{8,9},{9,8},{10,11... | collective-permute-start | bytes 786440 | tf_op jit(solution)/shard_map/ppermute | solution.py:26
  165.6 8.4 %collective-permute-start.22 = (bf16[128,1024]{1,0:T(8,128)(2,1)S(1)}, bf16[128,1024]{1,0:T(8,128)(2,1)S(1)}, u32[]{:S(2)}, u32[]{:S(2)}) collective-permute-start(bf16[128,1024]{1,0:T(8,128)(2,1)S(1)} %add_convert_fusion.8), channel_id=1, source_target_pairs={{0,2},{1,3},{2,4},{3,5},{4,6},{5,7},{6,0},{7,1},{8,10},{9,11},{10,... | collective-permute-start | bytes 786440 | tf_op jit(solution)/shard_map/ppermute | solution.py:30
  165.7 13.9 %collective-permute-start.38 = (bf16[128,1024]{1,0:T(8,128)(2,1)S(1)}, bf16[128,1024]{1,0:T(8,128)(2,1)S(1)}, u32[]{:S(2)}, u32[]{:S(2)}) collective-permute-start(bf16[128,1024]{1,0:T(8,128)(2,1)S(1)} %add_convert_fusion.5), channel_id=1, source_target_pairs={{0,2},{1,3},{2,4},{3,5},{4,6},{5,7},{6,0},{7,1},{8,10},{9,11},{10,... | collective-permute-start | bytes 786440 | tf_op jit(solution)/shard_map/ppermute | solution.py:30
  174.2 11.0 %collective-permute-start.25 = (bf16[128,1024]{1,0:T(8,128)(2,1)S(1)}, bf16[128,1024]{1,0:T(8,128)(2,1)S(1)}, u32[]{:S(2)}, u32[]{:S(2)}) collective-permute-start(bf16[128,1024]{1,0:T(8,128)(2,1)S(1)} %subtract_convert_fusion), channel_id=1, source_target_pairs={{0,2},{1,3},{2,4},{3,5},{4,6},{5,7},{6,0},{7,1},{8,11},{9,10},{10,... | collective-permute-start | bytes 786440 | tf_op jit(solution)/shard_map/ppermute | solution.py:38
  174.3 13.4 %collective-permute-start.24 = (bf16[128,1024]{1,0:T(8,128)(2,1)S(1)}, bf16[128,1024]{1,0:T(8,128)(2,1)S(1)}, u32[]{:S(2)}, u32[]{:S(2)}) collective-permute-start(bf16[128,1024]{1,0:T(8,128)(2,1)S(1)} %subtract_convert_fusion), channel_id=1, source_target_pairs={{0,1},{1,0},{2,3},{3,2},{4,5},{5,4},{6,7},{7,6},{8,9},{9,8},{10,11... | collective-permute-start | bytes 786440 | tf_op jit(solution)/shard_map/ppermute | solution.py:26
  179.8 13.6 %collective-permute-start.41 = (bf16[128,1024]{1,0:T(8,128)(2,1)S(1)}, bf16[128,1024]{1,0:T(8,128)(2,1)S(1)}, u32[]{:S(2)}, u32[]{:S(2)}) collective-permute-start(bf16[128,1024]{1,0:T(8,128)(2,1)S(1)} %add_convert_fusion.4), channel_id=1, source_target_pairs={{0,2},{1,3},{2,4},{3,5},{4,6},{5,7},{6,0},{7,1},{8,11},{9,10},{10,... | collective-permute-start | bytes 786440 | tf_op jit(solution)/shard_map/ppermute | solution.py:38
  179.9 11.4 %collective-permute-start.40 = (bf16[128,1024]{1,0:T(8,128)(2,1)S(1)}, bf16[128,1024]{1,0:T(8,128)(2,1)S(1)}, u32[]{:S(2)}, u32[]{:S(2)}) collective-permute-start(bf16[128,1024]{1,0:T(8,128)(2,1)S(1)} %add_convert_fusion.4), channel_id=1, source_target_pairs={{0,1},{1,0},{2,3},{3,2},{4,5},{5,4},{6,7},{7,6},{8,9},{9,8},{10,11... | collective-permute-start | bytes 786440 | tf_op jit(solution)/shard_map/ppermute | solution.py:26
  185.2 9.5 %collective-permute-start.29 = (bf16[128,1024]{1,0:T(8,128)(2,1)S(1)}, bf16[128,1024]{1,0:T(8,128)(2,1)S(1)}, u32[]{:S(2)}, u32[]{:S(2)}) collective-permute-start(bf16[128,1024]{1,0:T(8,128)(2,1)S(1)} %collective-permute-done.25.refs_4_), channel_id=1, source_target_pairs={{0,2},{1,3},{2,4},{3,5},{4,6},{5,7},{6,0},{7,1},{8,10},{9,11},{10,... | collective-permute-start | bytes 786440 | tf_op jit(solution)/shard_map/ppermute | solution.py:30
  185.3 11.0 %collective-permute-start.28 = (bf16[128,1024]{1,0:T(8,128)(2,1)S(1)}, bf16[128,1024]{1,0:T(8,128)(2,1)S(1)}, u32[]{:S(2)}, u32[]{:S(2)}) collective-permute-start(bf16[128,1024]{1,0:T(8,128)(2,1)S(1)} %collective-permute-done.25.refs_4_), channel_id=1, source_target_pairs={{0,1},{1,0},{2,3},{3,2},{4,5},{5,4},{6,7},{7,6},{8,9},{9,8},{10,11... | collective-permute-start | bytes 786440 | tf_op jit(solution)/shard_map/ppermute | solution.py:26
  189.5 119.5 %collective-permute-start.62 = (bf16[2752,128]{1,0:T(8,128)(2,1)S(1)}, bf16[2752,128]{1,0:T(8,128)(2,1)S(1)}, u32[]{:S(2)}, u32[]{:S(2)}) collective-permute-start(bf16[2752,128]{1,0:T(8,128)(2,1)S(1)} %get-tuple-element.71.refs_25_), channel_id=1, source_target_pairs={{0,8},{8,0},{16,24},{24,16},{1,9},{9,1},{17,25},{25,17},{2,10},{10... | collective-permute-start | bytes 2113544 | tf_op jit(solution)/shard_map/ppermute | solution.py:26
  191.3 118.2 %collective-permute-start.61 = (bf16[2752,128]{1,0:T(8,128)(2,1)S(1)}, bf16[2752,128]{1,0:T(8,128)(2,1)S(1)}, u32[]{:S(2)}, u32[]{:S(2)}) collective-permute-start(bf16[2752,128]{1,0:T(8,128)(2,1)S(1)} %get-tuple-element.72.refs_23_), channel_id=1, source_target_pairs={{0,8},{8,0},{16,24},{24,16},{1,9},{9,1},{17,25},{25,17},{2,10},{10... | collective-permute-start | bytes 2113544 | tf_op jit(solution)/shard_map/ppermute | solution.py:26
  193.4 116.2 %collective-permute-start.60 = (bf16[2752,128]{1,0:T(8,128)(2,1)S(1)}, bf16[2752,128]{1,0:T(8,128)(2,1)S(1)}, u32[]{:S(2)}, u32[]{:S(2)}) collective-permute-start(bf16[2752,128]{1,0:T(8,128)(2,1)S(1)} %get-tuple-element.73.refs_21_), channel_id=1, source_target_pairs={{0,8},{8,0},{16,24},{24,16},{1,9},{9,1},{17,25},{25,17},{2,10},{10... | collective-permute-start | bytes 2113544 | tf_op jit(solution)/shard_map/ppermute | solution.py:26
  194.8 20.3 %collective-permute-start.47 = (bf16[1376,128]{1,0:T(8,128)(2,1)S(1)}, bf16[1376,128]{1,0:T(8,128)(2,1)S(1)}, u32[]{:S(2)}, u32[]{:S(2)}) collective-permute-start(bf16[1376,128]{1,0:T(8,128)(2,1)S(1)} %pad_maximum_fusion.6), channel_id=1, source_target_pairs={{0,8},{8,0},{16,24},{24,16},{1,9},{9,1},{17,25},{25,17},{2,10},{10... | collective-permute-start | bytes 1056776 | tf_op jit(solution)/shard_map/ppermute | solution.py:26
  196.3 8.5 %collective-permute-start.42 = (bf16[128,1024]{1,0:T(8,128)(2,1)S(1)}, bf16[128,1024]{1,0:T(8,128)(2,1)S(1)}, u32[]{:S(2)}, u32[]{:S(2)}) collective-permute-start(bf16[128,1024]{1,0:T(8,128)(2,1)S(1)} %collective-permute-done.41.refs_12_), channel_id=1, source_target_pairs={{0,1},{1,0},{2,3},{3,2},{4,5},{5,4},{6,7},{7,6},{8,9},{9,8},{10,11... | collective-permute-start | bytes 786440 | tf_op jit(solution)/shard_map/ppermute | solution.py:26
  204.7 9.8 %collective-permute-start.43 = (bf16[128,1024]{1,0:T(8,128)(2,1)S(1)}, bf16[128,1024]{1,0:T(8,128)(2,1)S(1)}, u32[]{:S(2)}, u32[]{:S(2)}) collective-permute-start(bf16[128,1024]{1,0:T(8,128)(2,1)S(1)} %collective-permute-done.41.refs_12_), channel_id=1, source_target_pairs={{0,2},{1,3},{2,4},{3,5},{4,6},{5,7},{6,0},{7,1},{8,10},{9,11},{10,... | collective-permute-start | bytes 786440 | tf_op jit(solution)/shard_map/ppermute | solution.py:30
  214.5 34.7 %collective-permute-start.50 = (bf16[1376,128]{1,0:T(8,128)(2,1)S(1)}, bf16[1376,128]{1,0:T(8,128)(2,1)S(1)}, u32[]{:S(2)}, u32[]{:S(2)}) collective-permute-start(bf16[1376,128]{1,0:T(8,128)(2,1)S(1)} %pad_maximum_fusion.7), channel_id=1, source_target_pairs={{0,8},{8,0},{16,24},{24,16},{1,9},{9,1},{17,25},{25,17},{2,10},{10... | collective-permute-start | bytes 1056776 | tf_op jit(solution)/shard_map/ppermute | solution.py:26
  215.1 10.6 %collective-permute-start.31 = (bf16[128,1024]{1,0:T(8,128)(2,1)S(1)}, bf16[128,1024]{1,0:T(8,128)(2,1)S(1)}, u32[]{:S(2)}, u32[]{:S(2)}) collective-permute-start(bf16[128,1024]{1,0:T(8,128)(2,1)S(1)} %collective-permute-done.29.refs_6_), channel_id=1, source_target_pairs={{0,2},{1,3},{2,4},{3,5},{4,6},{5,7},{6,0},{7,1},{8,10},{9,11},{10,... | collective-permute-start | bytes 786440 | tf_op jit(solution)/shard_map/ppermute | solution.py:30
  225.6 7.9 %collective-permute-start.30 = (bf16[128,1024]{1,0:T(8,128)(2,1)S(1)}, bf16[128,1024]{1,0:T(8,128)(2,1)S(1)}, u32[]{:S(2)}, u32[]{:S(2)}) collective-permute-start(bf16[128,1024]{1,0:T(8,128)(2,1)S(1)} %collective-permute-done.29.refs_6_), channel_id=1, source_target_pairs={{0,1},{1,0},{2,3},{3,2},{4,5},{5,4},{6,7},{7,6},{8,9},{9,8},{10,11... | collective-permute-start | bytes 786440 | tf_op jit(solution)/shard_map/ppermute | solution.py:26
  233.5 7.0 %collective-permute-start.44 = (bf16[128,1024]{1,0:T(8,128)(2,1)S(1)}, bf16[128,1024]{1,0:T(8,128)(2,1)S(1)}, u32[]{:S(2)}, u32[]{:S(2)}) collective-permute-start(bf16[128,1024]{1,0:T(8,128)(2,1)S(1)} %collective-permute-done.43.refs_14_), channel_id=1, source_target_pairs={{0,1},{1,0},{2,3},{3,2},{4,5},{5,4},{6,7},{7,6},{8,9},{9,8},{10,11... | collective-permute-start | bytes 786440 | tf_op jit(solution)/shard_map/ppermute | solution.py:26
  240.5 8.2 %collective-permute-start.45 = (bf16[128,1024]{1,0:T(8,128)(2,1)S(1)}, bf16[128,1024]{1,0:T(8,128)(2,1)S(1)}, u32[]{:S(2)}, u32[]{:S(2)}) collective-permute-start(bf16[128,1024]{1,0:T(8,128)(2,1)S(1)} %collective-permute-done.43.refs_14_), channel_id=1, source_target_pairs={{0,2},{1,3},{2,4},{3,5},{4,6},{5,7},{6,0},{7,1},{8,10},{9,11},{10,... | collective-permute-start | bytes 786440 | tf_op jit(solution)/shard_map/ppermute | solution.py:30
  248.7 72.7 %collective-permute-start.59 = (bf16[2752,128]{1,0:T(8,128)(2,1)}, bf16[2752,128]{1,0:T(8,128)(2,1)}, u32[]{:S(2)}, u32[]{:S(2)}) collective-permute-start(bf16[2752,128]{1,0:T(8,128)(2,1)} %get-tuple-element.74.refs_19_), channel_id=1, source_target_pairs={{0,8},{8,0},{16,24},{24,16},{1,9},{9,1},{17,25},{25,17},{2,10},{10... | collective-permute-start | bytes 2113544 | tf_op jit(solution)/shard_map/ppermute | solution.py:26
  249.2 10.7 %collective-permute-start.48 = (bf16[1376,128]{1,0:T(8,128)(2,1)S(1)}, bf16[1376,128]{1,0:T(8,128)(2,1)S(1)}, u32[]{:S(2)}, u32[]{:S(2)}) collective-permute-start(bf16[1376,128]{1,0:T(8,128)(2,1)S(1)} %fusion.35), channel_id=1, source_target_pairs={{0,16},{8,24},{16,0},{24,8},{1,17},{9,25},{17,1},{25,9},{2,18},{10... | collective-permute-start | bytes 1056776 | tf_op jit(solution)/shard_map/ppermute | solution.py:30
  260.0 7.9 %collective-permute-start.32 = (bf16[128,1024]{1,0:T(8,128)(2,1)S(1)}, bf16[128,1024]{1,0:T(8,128)(2,1)S(1)}, u32[]{:S(2)}, u32[]{:S(2)}) collective-permute-start(bf16[128,1024]{1,0:T(8,128)(2,1)S(1)} %collective-permute-done.31.refs_8_), channel_id=1, source_target_pairs={{0,1},{1,0},{2,3},{3,2},{4,5},{5,4},{6,7},{7,6},{8,9},{9,8},{10,11... | collective-permute-start | bytes 786440 | tf_op jit(solution)/shard_map/ppermute | solution.py:26
  267.8 7.0 %collective-permute-start.46 = (bf16[128,1024]{1,0:T(8,128)(2,1)S(1)}, bf16[128,1024]{1,0:T(8,128)(2,1)S(1)}, u32[]{:S(2)}, u32[]{:S(2)}) collective-permute-start(bf16[128,1024]{1,0:T(8,128)(2,1)S(1)} %collective-permute-done.45.refs_16_), channel_id=1, source_target_pairs={{0,1},{1,0},{2,3},{3,2},{4,5},{5,4},{6,7},{7,6},{8,9},{9,8},{10,11... | collective-permute-start | bytes 786440 | tf_op jit(solution)/shard_map/ppermute | solution.py:26
  276.5 10.3 %collective-permute-start.51 = (bf16[1376,128]{1,0:T(8,128)(2,1)S(1)}, bf16[1376,128]{1,0:T(8,128)(2,1)S(1)}, u32[]{:S(2)}, u32[]{:S(2)}) collective-permute-start(bf16[1376,128]{1,0:T(8,128)(2,1)S(1)} %fusion.34), channel_id=1, source_target_pairs={{0,16},{8,24},{16,0},{24,8},{1,17},{9,25},{17,1},{25,9},{2,18},{10... | collective-permute-start | bytes 1056776 | tf_op jit(solution)/shard_map/ppermute | solution.py:30
  288.4 10.3 %collective-permute-start.54 = (bf16[1376,128]{1,0:T(8,128)(2,1)S(1)}, bf16[1376,128]{1,0:T(8,128)(2,1)S(1)}, u32[]{:S(2)}, u32[]{:S(2)}) collective-permute-start(bf16[1376,128]{1,0:T(8,128)(2,1)S(1)} %fusion.33), channel_id=1, source_target_pairs={{0,16},{8,24},{16,0},{24,8},{1,17},{9,25},{17,1},{25,9},{2,18},{10... | collective-permute-start | bytes 1056776 | tf_op jit(solution)/shard_map/ppermute | solution.py:30
  298.7 9.4 %collective-permute-start.57 = (bf16[1376,128]{1,0:T(8,128)(2,1)S(1)}, bf16[1376,128]{1,0:T(8,128)(2,1)S(1)}, u32[]{:S(2)}, u32[]{:S(2)}) collective-permute-start(bf16[1376,128]{1,0:T(8,128)(2,1)S(1)} %fusion.32), channel_id=1, source_target_pairs={{0,16},{8,24},{16,0},{24,8},{1,17},{9,25},{17,1},{25,9},{2,18},{10... | collective-permute-start | bytes 1056776 | tf_op jit(solution)/shard_map/ppermute | solution.py:30
  308.1 13.3 %collective-permute-start.49 = (bf16[1376,128]{1,0:T(8,128)(2,1)}, bf16[1376,128]{1,0:T(8,128)(2,1)}, u32[]{:S(2)}, u32[]{:S(2)}) collective-permute-start(bf16[1376,128]{1,0:T(8,128)(2,1)} %add_convert_fusion.3.refs_11_), channel_id=1, source_target_pairs={{0,8},{8,0},{16,24},{24,16},{1,9},{9,1},{17,25},{25,17},{2,10},{10... | collective-permute-start | bytes 1056776 | tf_op jit(solution)/shard_map/ppermute | solution.py:26
  309.0 12.4 %collective-permute-start.52 = (bf16[1376,128]{1,0:T(8,128)(2,1)}, bf16[1376,128]{1,0:T(8,128)(2,1)S(1)}, u32[]{:S(2)}, u32[]{:S(2)}) collective-permute-start(bf16[1376,128]{1,0:T(8,128)(2,1)} %add_convert_fusion.2.refs_13_), channel_id=1, source_target_pairs={{0,8},{8,0},{16,24},{24,16},{1,9},{9,1},{17,25},{25,17},{2,10},{10... | collective-permute-start | bytes 1056776 | tf_op jit(solution)/shard_map/ppermute | solution.py:26
  309.5 11.9 %collective-permute-start.55 = (bf16[1376,128]{1,0:T(8,128)(2,1)}, bf16[1376,128]{1,0:T(8,128)(2,1)S(1)}, u32[]{:S(2)}, u32[]{:S(2)}) collective-permute-start(bf16[1376,128]{1,0:T(8,128)(2,1)} %add_convert_fusion.1.refs_15_), channel_id=1, source_target_pairs={{0,8},{8,0},{16,24},{24,16},{1,9},{9,1},{17,25},{25,17},{2,10},{10... | collective-permute-start | bytes 1056776 | tf_op jit(solution)/shard_map/ppermute | solution.py:26
  311.2 10.2 %collective-permute-start.58 = (bf16[1376,128]{1,0:T(8,128)(2,1)}, bf16[1376,128]{1,0:T(8,128)(2,1)S(1)}, u32[]{:S(2)}, u32[]{:S(2)}) collective-permute-start(bf16[1376,128]{1,0:T(8,128)(2,1)} %add_convert_fusion.refs_17_), channel_id=1, source_target_pairs={{0,8},{8,0},{16,24},{24,16},{1,9},{9,1},{17,25},{25,17},{2,10},{10... | collective-permute-start | bytes 1056776 | tf_op jit(solution)/shard_map/ppermute | solution.py:26
  341.4 3.6 collective-permute-start.64
  345.0 3.6 collective-permute-start.65
  348.6 3.6 collective-permute-start.66
  352.2 4.5 %collective-permute-start.67 = (f32[8,128]{1,0:T(8,128)S(1)}, f32[8,128]{1,0:T(8,128)S(1)}, u32[]{:S(2)}, u32[]{:S(2)}) collective-permute-start(f32[8,128]{1,0:T(8,128)S(1)} %add.256), channel_id=1, source_target_pairs={{0,4},{1,5},{2,6},{3,7},{4,0},{5,1},{6,2},{7,3},{8,12},{9,13},{10,... | collective-permute-start | bytes 12296 | tf_op jit(solution)/shard_map/ppermute | solution.py:46
  (44 other events, 363.9 us)
